TPU v7x, 32 devices: a whole 2x2x4 slice. The times are simulated.
32 devices in a mesh: dp: 8 (over y, x, core), ctx: 4 (over z).
Axes of the slice: x: 2, y: 2, z: 4, core: 2. Of those that a mesh axis runs over, the one named last changes fastest.
Arguments:
- layer_in: bfloat16 [2, 8192, 768], P(None, ('dp', 'ctx')), may hold values from -6 to 6
- seg_start: int32 [2, 8192], P(None, ('dp', 'ctx')), may hold values from 0 to 964, as said below
- out_grad: bfloat16 [2, 8192, 768], P(None, ('dp', 'ctx')), may hold values from -6 to 6
- w_qkv: bfloat16 [768, 2304], P(('dp', 'ctx')), may hold values from -0.3125 to 0.3125
- w_attn_out: bfloat16 [768, 768], P(('dp', 'ctx')), may hold values from -0.75 to 0.75
- w_in: bfloat16 [768, 2304], P(('dp', 'ctx')), may hold values from -0.21875 to 0.21875
- w_mlp_out: bfloat16 [768, 1152], P(('dp', 'ctx')), may hold values from -0.1875 to 0.1875
- norm_attn: bfloat16 [768], P(('dp', 'ctx')), may hold values from 0.099609375 to 1.8984375
- norm_mlp: bfloat16 [768], P(('dp', 'ctx')), may hold values from 0.099609375 to 1.8984375
Outputs:
- layer_out: bfloat16 [2, 8192, 768], P(None, ('dp', 'ctx'))
- grad_in: bfloat16 [2, 8192, 768], P(None, ('dp', 'ctx'))
- grad_w_qkv: float32 [768, 2304], P(('dp', 'ctx'))
- grad_w_attn_out: float32 [768, 768], P(('dp', 'ctx'))
- grad_w_in: float32 [768, 2304], P(('dp', 'ctx'))
- grad_w_mlp_out: float32 [768, 1152], P(('dp', 'ctx'))
- grad_norm_attn: float32 [768], P(('dp', 'ctx'))
- grad_norm_mlp: float32 [768], P(('dp', 'ctx'))
Inputs may be any that keep to these rules, and one draw needn't show every extreme that they name: `seg_start`: documents are runs of 60 to 800 tokens that tile each sequence of 1024 tokens and never cross from one sequence to the next; every token of a document carries the position within its sequence of the document's first token, so the first token of each sequence carries 0.
All inputs are finite; a program needn't handle non-finite values.
Results may differ from a plain program's by a relative error of at most 0.017.
The roundings to bfloat16 on the way count: a program that leaves them out, or rounds other values in their place, can miss the bound.
Values may be sent and summed in bfloat16 or wider, within the bound.
A program may use at most 192 MiB of HBM per device.

v0:
```python
import jax
import jax.numpy as jnp
from jax import lax
from jax.sharding import PartitionSpec as P

HEADS = 12
HEAD_DIM = 64
FF = 1152


rope_base = 160000.0
norm_eps = 1e-05
neg_large = -1e30


def normalize(values):
    centered = values - jnp.mean(values, axis=-1, keepdims=True)
    spread = jnp.mean(centered * centered, axis=-1, keepdims=True)
    return centered * lax.rsqrt(spread + norm_eps)


def rope_tables(positions):
    half_dim = HEAD_DIM // 2
    frequency = rope_base ** (-(jnp.arange(half_dim).astype(jnp.float32) * 2.0) / HEAD_DIM)
    angles = positions.astype(jnp.float32)[:, None] * frequency[None, :]
    angles = jnp.concatenate([angles, angles], axis=-1)
    return (jnp.cos(angles), jnp.sin(angles))


def turn_half(values):
    half_dim = values.shape[-1] // 2
    return jnp.concatenate([-values[..., half_dim:], values[..., :half_dim]], axis=-1)


def rotate(values, cosine_table, sine_table):
    return values * cosine_table[:, None, :] + turn_half(values) * sine_table[:, None, :]


def unrotate(values, cosine_table, sine_table):
    return values * cosine_table[:, None, :] - turn_half(values) * sine_table[:, None, :]


def product(left, right):
    return jnp.dot(left, right, preferred_element_type=jnp.float32)


def left_transposed(left, right):
    return lax.dot_general(
        left, right, (((0,), (0,)), ((), ())), preferred_element_type=jnp.float32
    )


def right_transposed(left, right):
    return lax.dot_general(
        left, right, (((1,), (1,)), ((), ())), preferred_element_type=jnp.float32
    )


def to_groups(array):
    row_count, head_count, head_size = array.shape
    return array.reshape(row_count, head_count // 4, 4, head_size).transpose(1, 0, 2, 3)


def from_groups(array):
    group_count, row_count, group_heads, head_size = array.shape
    return array.transpose(1, 0, 2, 3).reshape(row_count, group_count * group_heads, head_size)


def attend_group(group_in, same_doc):
    query_part, key_part, value_part = group_in
    scores = jnp.einsum(
        "qhd,khd->hqk", query_part, key_part, preferred_element_type=jnp.float32
    ) * HEAD_DIM ** (-0.5)
    masked = jnp.where(same_doc[None], scores, neg_large)
    highest = jnp.max(masked, axis=-1, keepdims=True)
    shifted = jnp.exp(masked - highest)
    totals = jnp.sum(shifted, axis=-1, keepdims=True)
    attn_prob = shifted / totals
    log_total = highest + jnp.log(totals)
    mixed_out = jnp.einsum(
        "hqk,khd->qhd",
        attn_prob.astype(jnp.bfloat16),
        value_part,
        preferred_element_type=jnp.float32,
    )
    return (mixed_out, log_total[..., 0])


def attend_back(group_in, same_doc):
    query_part, key_part, value_part, grad_part, log_total = group_in
    scores = jnp.einsum(
        "qhd,khd->hqk", query_part, key_part, preferred_element_type=jnp.float32
    ) * HEAD_DIM ** (-0.5)
    attn_prob = jnp.where(same_doc[None], jnp.exp(scores - log_total[..., None]), 0.0)
    grad_prob = jnp.einsum(
        "qhd,khd->hqk", grad_part, value_part, preferred_element_type=jnp.float32
    )
    inner_sum = jnp.sum(attn_prob * grad_prob, axis=-1, keepdims=True)
    grad_score = (attn_prob * (grad_prob - inner_sum)).astype(jnp.bfloat16)
    grad_query = jnp.einsum(
        "hqk,khd->qhd", grad_score, key_part, preferred_element_type=jnp.float32
    ) * HEAD_DIM ** (-0.5)
    grad_key = jnp.einsum(
        "hqk,qhd->khd", grad_score, query_part, preferred_element_type=jnp.float32
    ) * HEAD_DIM ** (-0.5)
    grad_value = jnp.einsum(
        "hqk,qhd->khd",
        attn_prob.astype(jnp.bfloat16),
        grad_part,
        preferred_element_type=jnp.float32,
    )
    return (grad_query, grad_key, grad_value)


def scaled_norm(values_in, gain_row):
    return normalize(values_in) * gain_row


def geglu(first_half, second_half):
    return jax.nn.gelu(first_half, approximate=False) * second_half


def local(layer_in, seg_start, out_grad, w_qkv, w_attn_out, w_in, w_mlp_out, norm_attn, norm_mlp):
    micro_count = layer_in.shape[0]
    span_len = layer_in.shape[1]
    model_width = layer_in.shape[2]
    ctx_rank = lax.axis_index("ctx")
    grad_sums = (
        jnp.zeros((model_width, 3 * model_width), jnp.float32),
        jnp.zeros((model_width, model_width), jnp.float32),
        jnp.zeros((model_width, 2 * FF), jnp.float32),
        jnp.zeros((model_width, FF), jnp.float32),
        jnp.zeros((model_width,), jnp.float32),
        jnp.zeros((model_width,), jnp.float32),
    )
    offsets = ctx_rank * span_len + jnp.arange(span_len, dtype=jnp.int32)
    outputs = []
    grad_inputs = []
    for micro_step in range(micro_count):
        gathered = (
            lax.all_gather(w_qkv, ("dp", "ctx"), axis=0, tiled=True),
            lax.all_gather(w_attn_out, ("dp", "ctx"), axis=0, tiled=True),
            lax.all_gather(w_in, ("dp", "ctx"), axis=0, tiled=True),
            lax.all_gather(w_mlp_out, ("dp", "ctx"), axis=0, tiled=True),
            lax.all_gather(norm_attn, ("dp", "ctx"), axis=0, tiled=True),
            lax.all_gather(norm_mlp, ("dp", "ctx"), axis=0, tiled=True),
        )
        qkv_full, attn_full, in_full, mlp_full, gain_attn, gain_mlp = gathered
        starts_here = seg_start[micro_step]
        hidden = layer_in[micro_step].astype(jnp.float32)
        cosine_table, sine_table = rope_tables(offsets - starts_here)
        normed, norm_back = jax.vjp(scaled_norm, hidden, gain_attn.astype(jnp.float32))
        normed_low = normed.astype(jnp.bfloat16)
        qkv_local = product(normed_low, qkv_full).reshape(span_len, 3, HEADS, HEAD_DIM)
        queries = rotate(qkv_local[:, 0], cosine_table, sine_table).astype(jnp.bfloat16)
        keys_here = rotate(qkv_local[:, 1], cosine_table, sine_table).astype(jnp.bfloat16)
        values_here = qkv_local[:, 2].astype(jnp.bfloat16)
        keys_all, values_all, starts_all = (
            lax.all_gather(keys_here, "ctx", axis=0, tiled=True),
            lax.all_gather(values_here, "ctx", axis=0, tiled=True),
            lax.all_gather(starts_here, "ctx", axis=0, tiled=True),
        )
        same_doc = starts_here[:, None] == starts_all[None, :]
        query_groups = to_groups(queries)
        key_groups = to_groups(keys_all)
        value_groups = to_groups(values_all)
        mixed_out, log_total = lax.map(
            lambda group_in: attend_group(group_in, same_doc),
            (query_groups, key_groups, value_groups),
        )
        attended = from_groups(mixed_out).reshape(span_len, model_width).astype(jnp.bfloat16)
        middle = hidden + product(attended, attn_full)
        normed_mlp, norm_mlp_back = jax.vjp(scaled_norm, middle, gain_mlp.astype(jnp.float32))
        normed_mlp_low = normed_mlp.astype(jnp.bfloat16)
        projected = product(normed_mlp_low, in_full)
        gated_out, geglu_back = jax.vjp(geglu, projected[:, :FF], projected[:, FF:])
        gated_low = gated_out.astype(jnp.bfloat16)
        result = middle + right_transposed(gated_low, mlp_full)
        outputs.append(result.astype(jnp.bfloat16))
        qkv_full, attn_full, in_full, mlp_full = (
            lax.all_gather(w_qkv, ("dp", "ctx"), axis=0, tiled=True),
            lax.all_gather(w_attn_out, ("dp", "ctx"), axis=0, tiled=True),
            lax.all_gather(w_in, ("dp", "ctx"), axis=0, tiled=True),
            lax.all_gather(w_mlp_out, ("dp", "ctx"), axis=0, tiled=True),
        )
        grad_out = out_grad[micro_step].astype(jnp.float32)
        grad_out_low = out_grad[micro_step]
        grad_mlp_weight = left_transposed(grad_out_low, gated_low)
        grad_gated = product(grad_out_low, mlp_full)
        grad_first, grad_second = geglu_back(grad_gated)
        grad_projected = jnp.concatenate([grad_first, grad_second], axis=1).astype(jnp.bfloat16)
        grad_in_weight = left_transposed(normed_mlp_low, grad_projected)
        grad_normed_mlp = right_transposed(grad_projected, in_full)
        grad_middle_norm, grad_gain_mlp = norm_mlp_back(grad_normed_mlp)
        grad_middle = grad_out + grad_middle_norm
        grad_middle_low = grad_middle.astype(jnp.bfloat16)
        grad_attn_weight = left_transposed(attended, grad_middle_low)
        grad_attended = (
            right_transposed(grad_middle_low, attn_full)
            .astype(jnp.bfloat16)
            .reshape(span_len, HEADS, HEAD_DIM)
        )
        grad_groups = to_groups(grad_attended)
        grad_query_groups, grad_key_groups, grad_value_groups = lax.map(
            lambda group_in: attend_back(group_in, same_doc),
            (query_groups, key_groups, value_groups, grad_groups, log_total),
        )
        keys_total = keys_all.shape[0]
        grad_keys, grad_values = (
            lax.psum_scatter(
                from_groups(grad_key_groups).reshape(keys_total, model_width).astype(jnp.bfloat16),
                "ctx",
                scatter_dimension=0,
                tiled=True,
            ).astype(jnp.float32),
            lax.psum_scatter(
                from_groups(grad_value_groups)
                .reshape(keys_total, model_width)
                .astype(jnp.bfloat16),
                "ctx",
                scatter_dimension=0,
                tiled=True,
            ).astype(jnp.float32),
        )
        grad_qkv = jnp.stack(
            [
                unrotate(from_groups(grad_query_groups), cosine_table, sine_table),
                unrotate(grad_keys.reshape(span_len, HEADS, HEAD_DIM), cosine_table, sine_table),
                grad_values.reshape(span_len, HEADS, HEAD_DIM),
            ],
            axis=1,
        )
        grad_qkv = grad_qkv.reshape(span_len, 3 * model_width).astype(jnp.bfloat16)
        grad_qkv_weight = left_transposed(normed_low, grad_qkv)
        grad_normed = right_transposed(grad_qkv, qkv_full)
        grad_hidden_norm, grad_gain_attn = norm_back(grad_normed)
        grad_inputs.append((grad_middle + grad_hidden_norm).astype(jnp.bfloat16))
        grad_sums = (
            grad_sums[0] + grad_qkv_weight,
            grad_sums[1] + grad_attn_weight,
            grad_sums[2] + grad_in_weight,
            grad_sums[3] + grad_mlp_weight,
            grad_sums[4] + grad_gain_attn,
            grad_sums[5] + grad_gain_mlp,
        )
    shares = (
        lax.psum_scatter(grad_sums[0], ("dp", "ctx"), scatter_dimension=0, tiled=True),
        lax.psum_scatter(grad_sums[1], ("dp", "ctx"), scatter_dimension=0, tiled=True),
        lax.psum_scatter(grad_sums[2], ("dp", "ctx"), scatter_dimension=0, tiled=True),
        lax.psum_scatter(grad_sums[3], ("dp", "ctx"), scatter_dimension=0, tiled=True),
        lax.psum_scatter(grad_sums[4], ("dp", "ctx"), scatter_dimension=0, tiled=True),
        lax.psum_scatter(grad_sums[5], ("dp", "ctx"), scatter_dimension=0, tiled=True),
    )
    return (
        jnp.stack(outputs),
        jnp.stack(grad_inputs),
        shares[0],
        shares[1],
        shares[2],
        shares[3],
        shares[4],
        shares[5],
    )


def solution(mesh):
    return jax.shard_map(
        local,
        mesh=mesh,
        in_specs=(
            P(None, ("dp", "ctx"), None),
            P(None, ("dp", "ctx")),
            P(None, ("dp", "ctx"), None),
            P(("dp", "ctx"), None),
            P(("dp", "ctx"), None),
            P(("dp", "ctx"), None),
            P(("dp", "ctx"), None),
            P(("dp", "ctx")),
            P(("dp", "ctx")),
        ),
        out_specs=(
            P(None, ("dp", "ctx"), None),
            P(None, ("dp", "ctx"), None),
            P(("dp", "ctx"), None),
            P(("dp", "ctx"), None),
            P(("dp", "ctx"), None),
            P(("dp", "ctx"), None),
            P(("dp", "ctx")),
            P(("dp", "ctx")),
        ),
        check_vma=False,
    )
```

profile of v0, /device:TPU:0, one launch (start us, length us, event | category | flops | bytes accessed | tf_op | source)
XLA Modules:
  0.0 1121.6 jit_solution(3153288798120579650)
XLA Ops:
  9.6 42.7 %all-reduce.6 = (bf16[768]{0:T(1024)(128)(2,1)S(1)}, bf16[768]{0:T(1024)(128)(2,1)}) all-reduce(bf16[768]{0:T(1024)(128)(2,1)S(1)} %dynamic-update-slice, bf16[768]{0:T(1024)(128)(2,1)S(1)} %dynamic-update-slice.1), channel_id=1, replica_groups=mesh['dp'=8,'ctx'=4] {'dp','ctx'}, use_global_device_ids=true, to_apply=%add | all-reduce | flops 1536 | bytes 6144
  53.7 2.1 fusion.147
  56.4 17.2 %all-gather.13.cloned.1.call-done = bf16[768,2304]{1,0:T(8,128)(2,1)} async-done(((bf16[24,2304]{1,0:T(8,128)(2,1)}), bf16[768,2304]{1,0:T(8,128)(2,1)}) %all-gather.13.cloned.1.call-update) | async-done | bytes 3538960 | tf_op jit(solution)/shard_map/all_gather | solution.py:141
  73.6 4.5 copy.25
  78.1 2.2 fusion.182
  84.6 2.8 slice_bitcast_fusion
  87.4 2.1 fusion.164
  90.3 2.3 fusion.184
  94.8 2.5 slice_bitcast_fusion.1
  98.2 2.1 fusion.160
  102.5 10.2 all-gather.3
  112.7 8.2 all-gather.1
  122.6 34.2 %all-gather.23.cloned.1.call-done = bf16[1024,12,64]{0,2,1:T(8,128)(2,1)} async-done(((bf16[256,12,64]{0,2,1:T(8,128)(2,1)}), bf16[1024,12,64]{0,2,1:T(8,128)(2,1)}) %all-gather.23.cloned.1.call-update) | async-done | bytes 1572880 | tf_op jit(solution)/shard_map/all_gather | solution.py:159
  156.8 17.9 %while.57 = (s32[]{:T(128)}, bf16[3,256,4,64]{1,3,2,0:T(8,128)(2,1)S(1)}, f32[3,4,256]{2,1,0:T(4,128)S(1)}, bf16[3,1024,4,64]{1,3,2,0:T(8,128)(2,1)}, bf16[3,256...) while((s32[]{:T(128)}, ...), condition=%wide.region_13.14_spmd.clone, body=%wide.region_10.13_spmd.clone.sunk | while | flops 281279488 | bytes 15113321 | solution.py:167
  157.0 2.0 fusion.303
  160.3 2.4 fusion.305
  163.0 2.1 fusion.303
  166.3 2.4 fusion.305
  168.9 2.0 fusion.303
  172.2 2.4 fusion.305
  174.7 19.5 %all-gather.25.cloned.1.call-done = bf16[1024,1,12,64]{0,3,2,1:T(8,128)(2,1)} async-done(((bf16[256,1,12,64]{0,3,2,1:T(8,128)(2,1)}), bf16[1024,1,12,64]{0,3,2,1:T(8,128)(2,1)}) %all-gather.25.cloned.1.call-update) | async-done | bytes 1572880 | tf_op jit(solution)/shard_map/all_gather | solution.py:160
  194.2 37.4 %all-gather.15.cloned.1.call-done = bf16[1024,12,64]{0,2,1:T(8,128)(2,1)} async-done(((bf16[256,12,64]{0,2,1:T(8,128)(2,1)}), bf16[1024,12,64]{0,2,1:T(8,128)(2,1)}) %all-gather.15.cloned.1.call-update) | async-done | bytes 1572880 | tf_op jit(solution)/shard_map/all_gather | solution.py:159
  231.5 17.8 %while.56 = (s32[]{:T(128)}, bf16[3,256,4,64]{1,3,2,0:T(8,128)(2,1)S(1)}, f32[3,4,256]{2,1,0:T(4,128)S(1)}, bf16[3,1024,4,64]{1,3,2,0:T(8,128)(2,1)}, bf16[3,256...) while((s32[]{:T(128)}, ...), condition=%wide.region_5.6_spmd.clone, body=%wide.region_2.5_spmd.clone.sunk | while | flops 281279488 | bytes 15113321 | solution.py:167
  231.8 2.0 fusion.299
  235.0 2.4 fusion.301
  237.7 2.0 fusion.299
  241.0 2.4 fusion.301
  243.7 2.0 fusion.299
  246.9 2.4 fusion.301
  249.4 37.0 %all-gather.17.cloned.1.call-done = bf16[768,768]{1,0:T(8,128)(2,1)} async-done(((bf16[24,768]{1,0:T(8,128)(2,1)}), bf16[768,768]{1,0:T(8,128)(2,1)}) %all-gather.17.cloned.1.call-update) | async-done | bytes 1179664 | tf_op jit(solution)/shard_map/all_gather | solution.py:142
  286.4 1.9 fusion.226
  289.5 58.7 %all-gather.19.cloned.1.call-done = bf16[768,2304]{1,0:T(8,128)(2,1)} async-done(((bf16[24,2304]{1,0:T(8,128)(2,1)}), bf16[768,2304]{1,0:T(8,128)(2,1)}) %all-gather.19.cloned.1.call-update) | async-done | bytes 3538960 | tf_op jit(solution)/shard_map/all_gather | solution.py:143
  348.2 4.6 fusion.219
  352.8 52.6 %all-gather.21.cloned.1.call-done = bf16[768,1152]{1,0:T(8,128)(2,1)} async-done(((bf16[24,1152]{1,0:T(8,128)(2,1)}), bf16[768,1152]{1,0:T(8,128)(2,1)}) %all-gather.21.cloned.1.call-update) | async-done | bytes 1769488 | tf_op jit(solution)/shard_map/all_gather | solution.py:144
  405.4 5.5 add_convert_fusion
  415.1 3.1 add_convert_fusion.1
  430.8 36.4 %while.59 = (s32[]{:T(128)}, f32[3,256,4,64]{1,3,2,0:T(8,128)}, bf16[3,1024,4,64]{1,3,2,0:T(8,128)(2,1)}, bf16[3,1024,4,64]{1,3,2,0:T(8,128)(2,1)}, bf16[3,1024,...) while((s32[]{:T(128)}, f32[3,256,4,64]{1,3,2,0:T(8,128)}, ...), condition=%wide.region_29.30_spmd.clone, body=%wide.region_27.29_spmd.clone.sunk | while | flops 687406080 | bytes 63744296 | solution.py:204
  433.7 2.8 multiply_reduce_fusion.11
  445.7 2.8 multiply_reduce_fusion.11
  457.8 2.8 multiply_reduce_fusion.11
  469.8 2.0 copy.26
  475.5 33.2 %while.58 = (s32[]{:T(128)}, f32[3,256,4,64]{1,3,2,0:T(8,128)}, bf16[3,1024,4,64]{1,3,2,0:T(8,128)(2,1)}, bf16[3,1024,4,64]{1,3,2,0:T(8,128)(2,1)}, bf16[3,1024,...) while((s32[]{:T(128)}, f32[3,256,4,64]{1,3,2,0:T(8,128)}, ...), condition=%wide.region_20.21_spmd.clone, body=%wide.region_18.20_spmd.clone.sunk | while | flops 687406080 | bytes 63740172 | solution.py:204
  477.2 2.8 multiply_reduce_fusion.10
  488.3 2.8 multiply_reduce_fusion.10
  499.3 2.8 multiply_reduce_fusion.10
  511.2 2.5 fusion.114
  518.4 2.5 fusion.170
  521.0 4.1 convolution_add_fusion
  525.2 2.2 fusion.179
  528.3 2.0 convert_element_type.284
  530.3 13.0 %reduce-scatter.9.cloned.1.call-done = bf16[256,768]{0,1:T(8,128)(2,1)} async-done(((bf16[1024,768]{0,1:T(8,128)(2,1)}), bf16[256,768]{0,1:T(8,128)(2,1)}) %reduce-scatter.9.cloned.1.call-update) | async-done | bytes 393232 | tf_op jit(solution)/shard_map/reduce_scatter | solution.py:210
  546.2 33.8 %reduce-scatter.15.cloned.1.call-done = bf16[256,768]{0,1:T(8,128)(2,1)} async-done(((bf16[1024,768]{0,1:T(8,128)(2,1)}), bf16[256,768]{0,1:T(8,128)(2,1)}) %reduce-scatter.15.cloned.1.call-update) | async-done | bytes 393232 | tf_op jit(solution)/shard_map/reduce_scatter | solution.py:216
  579.9 2.4 maximum_convert_fusion.1
  583.6 32.8 %reduce-scatter.11.cloned.1.call-done = bf16[256,768]{0,1:T(8,128)(2,1)} async-done(((bf16[1024,768]{0,1:T(8,128)(2,1)}), bf16[256,768]{0,1:T(8,128)(2,1)}) %reduce-scatter.11.cloned.1.call-update) | async-done | bytes 393232 | tf_op jit(solution)/shard_map/reduce_scatter | solution.py:216
  619.4 4.2 convolution_add_fusion.1
  624.3 2.5 fusion.117
  628.6 131.8 %all-reduce.9.cloned.1.call-done = f32[768,1152]{0,1:T(8,128)} async-done(((f32[768,1152]{0,1:T(8,128)}), f32[768,1152]{0,1:T(8,128)}) %all-reduce.9.cloned.1.call-update) | async-done | bytes 3538960
  760.4 2.3 constant_dynamic-slice_fusion
  764.6 3.3 fusion.228
  770.3 39.8 %all-reduce.5 = (f32[768]{0:T(1024)S(1)}, f32[768]{0:T(1024)S(1)}) all-reduce(f32[768]{0:T(1024)S(1)} %add.197, f32[768]{0:T(1024)S(1)} %add.198), channel_id=14, replica_groups=mesh['dp'=8,'ctx'=4] {'dp','ctx'}, use_global_device_ids=true, to_apply=%region_40.41.clone | all-reduce | flops 1536 | bytes 12288
  811.3 2.1 fusion.174
  814.4 51.0 %reduce-scatter.19.cloned.1.call-done = f32[24,768]{1,0:T(8,128)} async-done(((f32[768,768]{1,0:T(8,128)}), f32[24,768]{1,0:T(8,128)}) %reduce-scatter.19.cloned.1.call-update) | async-done | bytes 73744 | tf_op jit(solution)/shard_map/reduce_scatter | solution.py:248
  865.3 124.7 %reduce-scatter.21.cloned.1.call-done = f32[24,2304]{1,0:T(8,128)} async-done(((f32[768,2304]{1,0:T(8,128)}), f32[24,2304]{1,0:T(8,128)}) %reduce-scatter.21.cloned.1.call-update) | async-done | bytes 221200 | tf_op jit(solution)/shard_map/reduce_scatter | solution.py:249
  990.0 124.6 %reduce-scatter.17.cloned.1.call-done = f32[24,2304]{1,0:T(8,128)} async-done(((f32[768,2304]{1,0:T(8,128)}), f32[24,2304]{1,0:T(8,128)}) %reduce-scatter.17.cloned.1.call-update) | async-done | bytes 221200 | tf_op jit(solution)/shard_map/reduce_scatter | solution.py:247
  (434 shorter events, 124.8 us)
Async XLA Ops:
  7.2 66.4 %all-gather.13.cloned.1.call-start = ((), (), s32[]{:S(2)}) async-start(), calls=%async_computation.7 | async-start | bytes 3649536 | tf_op jit(solution)/shard_map/all_gather | solution.py:141
  7.9 114.7 %all-gather.27.cloned.1.call-start = ((), (), s32[]{:S(2)}) async-start(), calls=%async_computation.21 | async-start | bytes 1966080 | tf_op jit(solution)/shard_map/all_gather | solution.py:160
  52.4 37.9 %copy-start.75 = (f32[768]{0:T(1024)}, f32[768]{0:T(1024)S(1)}, u32[]{:S(2)}) copy-start(f32[768]{0:T(1024)S(1)} %convert_element_type.236) | copy-start | bytes 9220
  53.7 24.4 %copy-start.86 = (f32[256]{0:T(256)}, f32[256]{0:T(256)S(1)}, u32[]{:S(2)}) copy-start(f32[256]{0:T(256)S(1)} %get-tuple-element.486) | copy-start | bytes 3076
  53.7 36.6 %copy-start.82 = (f32[256]{0:T(256)}, f32[256]{0:T(256)S(1)}, u32[]{:S(2)}) copy-start(f32[256]{0:T(256)S(1)} %get-tuple-element.487) | copy-start | bytes 3076
  56.4 21.7 %copy-start.92 = (f32[256]{0:T(256)}, f32[256]{0:T(256)S(1)}, u32[]{:S(2)}) copy-start(f32[256]{0:T(256)S(1)} %fusion.206) | copy-start | bytes 3076
  82.6 74.2 %all-gather.23.cloned.1.call-start = ((), (), s32[]{:S(2)}) async-start(), calls=%async_computation.12 | async-start | bytes 1966080 | tf_op jit(solution)/shard_map/all_gather | solution.py:159
  83.4 19.1 %copy-start.77 = (s32[1,256]{1,0:T(1,128)}, s32[1,256]{1,0:T(1,128)S(1)}, u32[]{:S(2)}) copy-start(s32[1,256]{1,0:T(1,128)S(1)} %get-tuple-element.475) | copy-start | bytes 3076
  84.6 2.8 copy-start.66
  84.6 2.8 copy-start.69
  89.5 104.6 %all-gather.25.cloned.1.call-start = ((), (), s32[]{:S(2)}) async-start(), calls=%async_computation.20 | async-start | bytes 1966080 | tf_op jit(solution)/shard_map/all_gather | solution.py:160
  94.8 136.8 %all-gather.15.cloned.1.call-start = ((), (), s32[]{:S(2)}) async-start(), calls=%async_computation.8 | async-start | bytes 1966080 | tf_op jit(solution)/shard_map/all_gather | solution.py:159
  98.2 22.8 %copy-start.107 = (bf16[768]{0:T(1024)(128)(2,1)S(1)}, bf16[768]{0:T(1024)(128)(2,1)}, u32[]{:S(2)}) copy-start(bf16[768]{0:T(1024)(128)(2,1)} %get-tuple-element.413) | copy-start | bytes 4612
  98.2 22.8 %copy-start.48 = (f32[256,12,64]{0,2,1:T(8,128)S(1)}, f32[256,12,64]{0,2,1:T(8,128)}, u32[]{:S(2)}) copy-start(f32[256,12,64]{0,2,1:T(8,128)} %get-tuple-element.438) | copy-start | bytes 2359300
  100.3 186.1 %all-gather.17.cloned.1.call-start = ((), (), s32[]{:S(2)}) async-start(), calls=%async_computation.9 | async-start | bytes 1216512 | tf_op jit(solution)/shard_map/all_gather | solution.py:142
  100.9 247.3 %all-gather.19.cloned.1.call-start = ((), (), s32[]{:S(2)}) async-start(), calls=%async_computation.10 | async-start | bytes 3649536 | tf_op jit(solution)/shard_map/all_gather | solution.py:143
  101.6 303.8 %all-gather.21.cloned.1.call-start = ((), (), s32[]{:S(2)}) async-start(), calls=%async_computation.11 | async-start | bytes 1824768 | tf_op jit(solution)/shard_map/all_gather | solution.py:144
  102.4 425.9 %reduce-scatter.13.cloned.1.call-start = ((), (), s32[]{:S(2)}) async-start(), calls=%async_computation.15 | async-start | bytes 1966080 | tf_op jit(solution)/shard_map/reduce_scatter | solution.py:210
  122.2 34.6 %copy-start.78 = (s32[1,256]{1,0:T(1,128)S(1)}, s32[1,256]{1,0:T(1,128)}, u32[]{:S(2)}) copy-start(s32[1,256]{1,0:T(1,128)} %copy-done.77) | copy-start | bytes 3076
  174.7 56.9 %copy-start.10 = (bf16[3,256,4,64]{1,3,2,0:T(8,128)(2,1)}, bf16[3,256,4,64]{1,3,2,0:T(8,128)(2,1)S(1)}, u32[]{:S(2)}) copy-start(bf16[3,256,4,64]{1,3,2,0:T(8,128)(2,1)S(1)} %get-tuple-element.893) | copy-start | bytes 1179652
  174.7 56.9 %copy-start.80 = (f32[3,4,256]{2,1,0:T(4,128)}, f32[3,4,256]{2,1,0:T(4,128)S(1)}, u32[]{:S(2)}) copy-start(f32[3,4,256]{2,1,0:T(4,128)S(1)} %get-tuple-element.798) | copy-start | bytes 36868
  174.7 111.7 %copy-start.32 = (bf16[3,256,4,64]{1,3,2,0:T(8,128)(2,1)}, bf16[3,256,4,64]{1,3,2,0:T(8,128)(2,1)S(1)}, u32[]{:S(2)}) copy-start(bf16[3,256,4,64]{1,3,2,0:T(8,128)(2,1)S(1)} %get-tuple-element.193) | copy-start | bytes 1179652
  231.5 54.9 %copy-start = (bf16[2,256,768]{2,1,0:T(8,128)(2,1)S(1)}, bf16[2,256,768]{2,1,0:T(8,128)(2,1)}, u32[]{:S(2)}) copy-start(bf16[2,256,768]{2,1,0:T(8,128)(2,1)} %param.17) | copy-start | bytes 2359300
  249.4 39.2 %copy-start.81 = (f32[3,4,256]{2,1,0:T(4,128)}, f32[3,4,256]{2,1,0:T(4,128)S(1)}, u32[]{:S(2)}) copy-start(f32[3,4,256]{2,1,0:T(4,128)S(1)} %get-tuple-element.834) | copy-start | bytes 36868
  249.4 39.2 %copy-start.41 = (bf16[3,256,4,64]{1,3,2,0:T(8,128)(2,1)}, bf16[3,256,4,64]{1,3,2,0:T(8,128)(2,1)S(1)}, u32[]{:S(2)}) copy-start(bf16[3,256,4,64]{1,3,2,0:T(8,128)(2,1)S(1)} %get-tuple-element.192) | copy-start | bytes 1179652
  288.4 132.1 %copy-start.88 = (f32[256]{0:T(256)}, f32[256]{0:T(256)S(1)}, u32[]{:S(2)}) copy-start(f32[256]{0:T(256)S(1)} %broadcast_multiply_fusion.2) | copy-start | bytes 3076
  289.2 131.3 %copy-start.90 = (f32[256]{0:T(256)}, f32[256]{0:T(256)S(1)}, u32[]{:S(2)}) copy-start(f32[256]{0:T(256)S(1)} %broadcast_multiply_fusion.4) | copy-start | bytes 3076
  289.5 131.1 %copy-start.94 = (f32[256]{0:T(256)}, f32[256]{0:T(256)S(1)}, u32[]{:S(2)}) copy-start(f32[256]{0:T(256)S(1)} %fusion.207) | copy-start | bytes 3076
  289.5 131.0 %copy-start.96 = (f32[256]{0:T(256)}, f32[256]{0:T(256)S(1)}, u32[]{:S(2)}) copy-start(f32[256]{0:T(256)S(1)} %fusion.205) | copy-start | bytes 3076
  289.5 115.9 %copy-start.14 = (bf16[2,256,768]{2,1,0:T(8,128)(2,1)S(1)}, bf16[2,256,768]{2,1,0:T(8,128)(2,1)}, u32[]{:S(2)}) copy-start(bf16[2,256,768]{2,1,0:T(8,128)(2,1)} %param.19) | copy-start | bytes 2359300
  405.4 5.5 copy-start.11
  410.9 8.4 copy-start.72
  413.4 6.0 copy-start.55
  428.2 2.7 copy-start.3
  431.1 2.6 copy-start.54
  443.1 2.6 copy-start.54
  455.2 2.6 copy-start.54
  467.2 76.1 %reduce-scatter.9.cloned.1.call-start = ((), (), s32[]{:S(2)}) async-start(), calls=%async_computation.13 | async-start | bytes 1966080 | tf_op jit(solution)/shard_map/reduce_scatter | solution.py:210
  472.8 2.8 copy-start.2
  508.7 71.2 %reduce-scatter.15.cloned.1.call-start = ((), (), s32[]{:S(2)}) async-start(), calls=%async_computation.16 | async-start | bytes 1966080 | tf_op jit(solution)/shard_map/reduce_scatter | solution.py:216
  509.5 106.9 %reduce-scatter.11.cloned.1.call-start = ((), (), s32[]{:S(2)}) async-start(), calls=%async_computation.14 | async-start | bytes 1966080 | tf_op jit(solution)/shard_map/reduce_scatter | solution.py:216
  510.1 250.3 %all-reduce.9.cloned.1.call-start = ((), (), s32[]{:S(2)}) async-start(), calls=%async_computation.22 | async-start | bytes 7077888
  513.7 351.6 %reduce-scatter.19.cloned.1.call-start = ((), (), s32[]{:S(2)}) async-start(), calls=%async_computation.18 | async-start | bytes 2433024 | tf_op jit(solution)/shard_map/reduce_scatter | solution.py:248
  517.7 3.2 copy-start.56
  517.8 3.2 copy-start.89
  517.8 3.2 copy-start.95
  517.8 472.3 %reduce-scatter.21.cloned.1.call-start = ((), (), s32[]{:S(2)}) async-start(), calls=%async_computation.19 | async-start | bytes 7299072 | tf_op jit(solution)/shard_map/reduce_scatter | solution.py:249
  518.4 2.6 copy-start.73
  525.1 589.5 %reduce-scatter.17.cloned.1.call-start = ((), (), s32[]{:S(2)}) async-start(), calls=%async_computation.17 | async-start | bytes 7299072 | tf_op jit(solution)/shard_map/reduce_scatter | solution.py:247
  579.9 2.5 copy-start.63
  579.9 2.5 copy-start.65
  583.6 34.1 %copy-start.1 = (bf16[2,256,768]{2,1,0:T(8,128)(2,1)S(1)}, bf16[2,256,768]{2,1,0:T(8,128)(2,1)}, u32[]{:S(2)}) copy-start(bf16[2,256,768]{2,1,0:T(8,128)(2,1)} %param.17) | copy-start | bytes 2359300
  583.6 34.1 %copy-start.76 = (f32[768]{0:T(1024)S(1)}, f32[768]{0:T(1024)}, u32[]{:S(2)}) copy-start(f32[768]{0:T(1024)} %copy-done.75) | copy-start | bytes 9220
  583.6 34.1 %copy-start.83 = (f32[256]{0:T(256)S(1)}, f32[256]{0:T(256)}, u32[]{:S(2)}) copy-start(f32[256]{0:T(256)} %copy-done.82) | copy-start | bytes 3076
  583.6 34.1 %copy-start.85 = (f32[256]{0:T(256)S(1)}, f32[256]{0:T(256)}, u32[]{:S(2)}) copy-start(f32[256]{0:T(256)} %copy-done.84) | copy-start | bytes 3076
  624.3 2.5 copy-start.13
  624.3 2.6 copy-start.35
  627.6 137.0 %copy-start.38 = (bf16[256,3,12,64]{0,3,2,1:T(8,128)(2,1)S(1)}, bf16[256,3,12,64]{0,3,2,1:T(8,128)(2,1)}, u32[]{:S(2)}) copy-start(bf16[256,3,12,64]{0,3,2,1:T(8,128)(2,1)} %maximum_convert_fusion.1) | copy-start | bytes 3538948
  764.6 3.3 copy-start.40
  764.6 3.4 copy-start.43
  769.4 41.9 %copy-start.21 = (f32[256,768]{1,0:T(8,128)S(1)}, f32[256,768]{1,0:T(8,128)}, u32[]{:S(2)}) copy-start(f32[256,768]{1,0:T(8,128)} %copy-done.20) | copy-start | bytes 2359300
  769.4 41.9 %copy-start.23 = (f32[256,768]{1,0:T(8,128)S(1)}, f32[256,768]{1,0:T(8,128)}, u32[]{:S(2)}) copy-start(f32[256,768]{1,0:T(8,128)} %copy-done.22) | copy-start | bytes 2359300
  769.4 41.9 %copy-start.99 = (f32[256]{0:T(256)S(1)}, f32[256]{0:T(256)}, u32[]{:S(2)}) copy-start(f32[256]{0:T(256)} %copy-done.98) | copy-start | bytes 3076
  769.5 41.9 %copy-start.101 = (f32[256]{0:T(256)S(1)}, f32[256]{0:T(256)}, u32[]{:S(2)}) copy-start(f32[256]{0:T(256)} %copy-done.100) | copy-start | bytes 3076
  (82 other events, 120.7 us)
Sparse Core Ops, SparseCore 0:
  10.8 62.7 all-gather.12
  82.7 36.5 all-gather.26
  120.9 35.9 all-gather.22
  158.2 35.9 all-gather.24
  195.6 35.9 all-gather.14
  234.2 52.1 all-gather.16
  289.2 58.9 all-gather.18
  351.0 54.3 all-gather.20
  467.4 34.4 reduce-scatter.12
  508.9 34.4 reduce-scatter.8
  545.6 34.2 reduce-scatter.14
  582.1 34.2 reduce-scatter.10
  622.0 138.3 all-reduce.8
  766.1 99.1 reduce-scatter.18
  871.4 118.5 reduce-scatter.20
  996.1 118.4 reduce-scatter.16
where the time goes:
time: 1130 us; the launch traced here: 1120 us
  waiting for transfers between devices  772 us (68%)
  matrix products  124 us (11%)
  blocking collectives  101 us (9%)
  local copies, waits for them, and re-layouts  57 us (5%)
  other arithmetic  50.2 us (4%)
  between operations  15.5 us (1%)
    unnamed x17, waiting for transfers between devices  136 us
    reduce_scatter x1, waiting for transfers between devices, local(): lax.psum_scatter(grad_sums[2], ('dp', 'ctx'), scatter_dimension=0, tiled=...  125 us
    reduce_scatter x1, waiting for transfers between devices, local(): lax.psum_scatter(grad_sums[0], ('dp', 'ctx'), scatter_dimension=0, tiled=...  125 us
    unnamed x2, blocking collectives  82.5 us
    all_gather x2, waiting for transfers between devices, local(): lax.all_gather(keys_here, 'ctx', axis=0, tiled=True)  71.6 us
    reduce_scatter x2, waiting for transfers between devices, local(): lax.psum_scatter(from_groups(grad_value_groups).reshape(keys_total, model...  66.5 us
    all_gather x1, waiting for transfers between devices, local(): lax.all_gather(w_in, ('dp', 'ctx'), axis=0, tiled=True)  58.7 us
    all_gather x1, waiting for transfers between devices, local(): lax.all_gather(w_mlp_out, ('dp', 'ctx'), axis=0, tiled=True)  52.6 us
  transfers between devices with their start and end apart: 16, of which 14 were waited for; matrix products, arithmetic and copies ran while one was open for 13% of the time, Pallas kernels for 0%

commit v1 on v0

--- a/solution.py
+++ b/solution.py
@@ -1,16 +1,701 @@
+import functools
 import jax
 import jax.numpy as jnp
 from jax import lax
+from jax.experimental import pallas as pl
+from jax.experimental.pallas import tpu as pltpu
 from jax.sharding import PartitionSpec as P
+
+MESH = pl.DeviceIdType.MESH
+bf16 = jnp.bfloat16
+f32 = jnp.float32
 
 HEADS = 12
 HEAD_DIM = 64
 FF = 1152
-
-
 rope_base = 160000.0
 norm_eps = 1e-05
 neg_large = -1e30
+
+WIDTH = 3456
+GATHER = [(0, 512), (512, 768), (1280, 384), (1664, 640), (2304, 512), (2816, 640)]
+PAIR = 128
+ATTN = 1280
+IN = 1664
+MLP = 2816
+REDUCE = {
+    "m": (2816, 640),
+    "i0": (1664, 640),
+    "i1": (2304, 512),
+    "a": (1280, 384),
+    "q2": (896, 384),
+    "q1": (512, 384),
+    "q0": (128, 384),
+    "g": (0, 128),
+}
+
+
+def dims(left, right, left_at, right_at):
+    return lax.dot_general(
+        left, right, (((left_at,), (right_at,)), ((), ())), preferred_element_type=f32
+    )
+
+
+def times(left, right):
+    return jnp.dot(left, right, preferred_element_type=f32)
+
+
+def step_kernel(
+    x_in, dy_in, seg_in, wp, freq,
+    lo_out, gi_out, gp_out, land, keep,
+    xs, dys, sg, h1t, wq, wa, wi, wm, gains, cosr, sinr, qk, big, probs, otb, rl, x1, h2, hid, hidp,
+    dgo, dgp, dx1b, dx1bp, dot_send, dot_own, f1r, lo, gi, grad, grow, dkb, dvb,
+    ra, rb, ra2, rb2, zs, zp, zm, zx, fin,
+    rs_, ls_, sends,
+):
+    dp = lax.axis_index("dp")
+    z = lax.axis_index("ctx")
+    q = dp // 2
+    k = lax.rem(dp, 2)
+    other = 1 - k
+    pn = dp + 1 - 2 * k
+    xn = dp + 2 - 4 * lax.rem(dp // 2, 2)
+    yn = dp + 4 - 8 * (dp // 4)
+    zn = z + 1 - 2 * lax.rem(z, 2)
+    zb = jnp.where(z < 2, 2, 1)
+    zh = z // 2
+    qx = q + 1 - 2 * lax.rem(q, 2)
+    qy = q + 2 - 4 * (q // 2)
+    qd = qx + 2 - 4 * (qx // 2)
+    inner = jnp.logical_or(z == 1, z == 2)
+    outer = jnp.logical_or(z == 0, z == 3)
+    names = {}
+    count = {"send": 0, "local": 0}
+    drains = []
+
+    def rsem(name):
+        return rs_.at[names.setdefault(name, len(names))]
+
+    def send(src, dst, name, dev, when=None):
+        i = count["send"]
+        count["send"] += 1
+        copy = pltpu.make_async_remote_copy(
+            src_ref=src, dst_ref=dst, send_sem=sends.at[i], recv_sem=rsem(name),
+            device_id=dev, device_id_type=MESH,
+        )
+        if when is None:
+            copy.start()
+            drains.append(copy.wait_send)
+        else:
+            pl.when(when)(copy.start)
+            drains.append(lambda: pl.when(when)(copy.wait_send))
+
+    def local(src, dst, name):
+        copy = pltpu.make_async_copy(src, dst, rsem(name))
+        copy.start()
+        return copy
+
+    def arrived(ref, name):
+        pltpu.make_async_copy(ref, ref, rsem(name)).wait()
+
+    def rows(start, size):
+        return pl.ds(pl.multiple_of(start, 8), size)
+
+    def lanes(start, size):
+        return pl.ds(pl.multiple_of(start, 128), size)
+
+    barrier = pltpu.get_barrier_semaphore()
+    for dz in range(1, 4):
+        for kk in range(2):
+            pl.semaphore_signal(
+                barrier, inc=1, device_id=(2 * q + kk, lax.rem(z + dz, 4)), device_id_type=MESH
+            )
+    for dev in (pn, xn, yn):
+        pl.semaphore_signal(barrier, inc=1, device_id=(dev, z), device_id_type=MESH)
+    pl.semaphore_wait(barrier, 9)
+
+    def zstage(u):
+        o, w = GATHER[u]
+        cols = pl.ds(o, w)
+        dst = land.at[rows(dp * 96 + z * 24, 24), cols]
+        for c in range(2):
+            src = wp.at[c, :, cols]
+            send(src, dst, f"z{u}", (2 * q + c, zn))
+            send(src, dst, f"z{u}", (2 * q + c, zb))
+            send(src, dst, f"z{u}", (pn, z), when=k != c)
+            pl.when(k == c)(lambda src=src: local(src, dst, f"z{u}") and None)
+
+    def xystage(u):
+        o, w = GATHER[u]
+        cols = pl.ds(o, w)
+        slab = land.at[rows(q * 192, 192), cols]
+        arrived(slab, f"z{u}")
+        send(slab, slab, f"x{u}", (xn, z))
+        send(slab, slab, f"y{u}", (yn, z))
+        for j in range(2):
+            part = land.at[rows((2 * q + j) * 96 + lax.rem(4 - 2 * z + 4, 4) * 24, 48), cols]
+            send(part, part, f"z{u}", (dp, zn), when=inner)
+
+    def diag(u):
+        o, w = GATHER[u]
+        cols = pl.ds(o, w)
+        arrived(land.at[rows(qx * 192, 192), cols], f"x{u}")
+        part = land.at[rows(qx * 192, 96), cols]
+        send(part, part, f"dx{u}", (yn, z))
+        arrived(land.at[rows(qy * 192, 192), cols], f"y{u}")
+        part = land.at[rows(qy * 192 + 96, 96), cols]
+        send(part, part, f"dy{u}", (xn, z))
+
+    def done(u):
+        o, w = GATHER[u]
+        cols = pl.ds(o, w)
+        arrived(land.at[rows(qd * 192, 96), cols], f"dx{u}")
+        arrived(land.at[rows(qd * 192 + 96, 96), cols], f"dy{u}")
+
+    def activation(src_ref, dst_ref, name):
+        for m in range(2):
+            to = 2 * k + m
+            src = src_ref.at[m]
+            dst = dst_ref.at[rows(z * 256, 256), :]
+            sem = rs_.at[base[name] + lax.rem(z, 2)]
+            i = count["send"]
+            count["send"] += 1
+            copy = pltpu.make_async_remote_copy(
+                src_ref=src, dst_ref=dst, send_sem=sends.at[i], recv_sem=sem,
+                device_id=(2 * q + zh, to), device_id_type=MESH,
+            )
+            pl.when(to != z)(copy.start)
+            pl.when(to == z)(pltpu.make_async_copy(src, dst, sem).start)
+            drains.append(lambda copy=copy, to=to: pl.when(to != z)(copy.wait_send))
+
+    base = {}
+    for name in ("ax", "ay", "alo", "agi"):
+        base[name] = len(names)
+        names[name + "0"] = len(names)
+        names[name + "1"] = len(names)
+
+    def share_activation(ref, name):
+        for j in range(2):
+            r = rows(k * 512 + j * 256, 256)
+            arrived(ref.at[r, :], f"{name}{j}")
+            send(ref.at[r, :], ref.at[r, :], f"p{name}{j}", (pn, z))
+
+    def shared_activation(ref, name):
+        for j in range(2):
+            arrived(ref.at[rows(other * 512 + j * 256, 256), :], f"p{name}{j}")
+
+    def give_back(src_ref, out_ref, name):
+        m = lax.rem(z, 2)
+        for j in range(2):
+            to = 2 * k + j
+            src = src_ref.at[pl.ds(j * 256, 256), :]
+            dst = out_ref.at[m]
+            sem = rs_.at[base[name] + m]
+            i = count["send"]
+            count["send"] += 1
+            copy = pltpu.make_async_remote_copy(
+                src_ref=src, dst_ref=dst, send_sem=sends.at[i], recv_sem=sem,
+                device_id=(2 * q + zh, to), device_id_type=MESH,
+            )
+            here = jnp.logical_and(to == z, zh == k)
+            away = jnp.logical_not(here)
+            pl.when(away)(copy.start)
+            pl.when(here)(pltpu.make_async_copy(src, dst, sem).start)
+            drains.append(lambda copy=copy, away=away: pl.when(away)(copy.wait_send))
+
+    def given_back(out_ref, name):
+        for m in range(2):
+            arrived(out_ref.at[m], f"{name}{m}")
+
+    def seg_send():
+        for m in range(2):
+            to = 2 * k + m
+            src = seg_in.at[m]
+            dst = sg.at[:, lanes(z * 256, 256)]
+            for c in range(2):
+                i = count["send"]
+                count["send"] += 1
+                copy = pltpu.make_async_remote_copy(
+                    src_ref=src, dst_ref=dst, send_sem=sends.at[i], recv_sem=rsem("seg"),
+                    device_id=(2 * q + c, to), device_id_type=MESH,
+                )
+                here = jnp.logical_and(to == z, k == c)
+                away = jnp.logical_not(here)
+                pl.when(away)(copy.start)
+                pl.when(here)(pltpu.make_async_copy(src, dst, rsem("seg")).start)
+                drains.append(lambda copy=copy, away=away: pl.when(away)(copy.wait_send))
+
+    def s1(u):
+        o, w = REDUCE[u]
+        cols = pl.ds(o, w)
+        for slot, quarter in enumerate((qx, qd)):
+            send(grad.at[rows(quarter * 192, 96), cols], ra.at[slot, :, cols], f"ra{u}", (xn, z))
+        for slot, quarter in enumerate((qy, qd)):
+            send(grad.at[rows(quarter * 192 + 96, 96), cols], rb.at[slot, :, cols], f"rb{u}", (yn, z))
+
+    def s2(u):
+        o, w = REDUCE[u]
+        cols = pl.ds(o, w)
+        arrived(ra.at[:, :, cols], f"ra{u}")
+        r = rows(qy * 192, 96)
+        grad[r, cols] = (grad[r, cols].astype(f32) + ra[1, :, cols].astype(f32)).astype(bf16)
+        send(grad.at[r, cols], ra2.at[:, cols], f"ra2{u}", (yn, z))
+        arrived(rb.at[:, :, cols], f"rb{u}")
+        r2 = rows(qx * 192 + 96, 96)
+        grad[r2, cols] = (grad[r2, cols].astype(f32) + rb[1, :, cols].astype(f32)).astype(bf16)
+        send(grad.at[r2, cols], rb2.at[:, cols], f"rb2{u}", (xn, z))
+
+    def s3(u):
+        o, w = REDUCE[u]
+        cols = pl.ds(o, w)
+        arrived(ra2.at[:, cols], f"ra2{u}")
+        arrived(rb2.at[:, cols], f"rb2{u}")
+        for j, (one, two) in enumerate(((ra, ra2), (rb, rb2))):
+            total = (
+                grad[rows(q * 192 + 96 * j, 96), cols].astype(f32)
+                + one[0, :, cols].astype(f32)
+                + two[:, cols].astype(f32)
+            )
+            for at in range(4):
+                zs[j, at, :, cols] = total[24 * at : 24 * at + 24].astype(bf16)
+        send(zs.at[:, zn, :, cols], zp.at[:, :, cols], f"zp{u}", (dp, zn))
+        far = 2 * (1 - zh)
+        send(zs.at[:, pl.ds(far, 2), :, cols], zm.at[:, :, :, cols], f"zm{u}", (dp, zn), when=outer)
+
+    def s4(u):
+        o, w = REDUCE[u]
+        cols = pl.ds(o, w)
+        far = 2 * (1 - zh)
+
+        @pl.when(inner)
+        def _():
+            arrived(zm.at[:, :, :, cols], f"zm{u}")
+            for j in range(2):
+                for at in range(2):
+                    zs[j, far + at, :, cols] = (
+                        zs[j, far + at, :, cols].astype(f32) + zm[j, at, :, cols].astype(f32)
+                    ).astype(bf16)
+
+        for at in range(2):
+            send(zs.at[:, far + at, :, cols], zx.at[:, :, cols], f"zx{u}", (dp, far + at), when=inner)
+
+    def s5(u):
+        o, w = REDUCE[u]
+        cols = pl.ds(o, w)
+        arrived(zp.at[:, :, cols], f"zp{u}")
+        arrived(zx.at[:, :, cols], f"zx{u}")
+        for j in range(2):
+            fin[j, :, cols] = (
+                zs[j, z, :, cols].astype(f32) + zp[j, :, cols].astype(f32) + zx[j, :, cols].astype(f32)
+            )
+        local(fin.at[k, :, cols], gp_out.at[k, :, cols], f"fl{u}")
+        send(fin.at[other, :, cols], gp_out.at[k, :, cols], f"fr{u}", (pn, z))
+
+    def s6(u):
+        o, w = REDUCE[u]
+        cols = pl.ds(o, w)
+        arrived(gp_out.at[k, :, cols], f"fl{u}")
+        arrived(gp_out.at[other, :, cols], f"fr{u}")
+
+    zstage(0)
+    activation(x_in, xs, "ax")
+    seg_send()
+    zstage(1)
+    xystage(0)
+    share_activation(xs, "ax")
+    xystage(1)
+    zstage(2)
+    zstage(3)
+    arrived(sg, "seg")
+    positions = (lax.broadcasted_iota(jnp.int32, (1, 1024), 1) - sg[...]).astype(f32)
+    angles = freq[:, 0:1] * positions
+    cosr[...] = jnp.cos(angles)
+    sinr[...] = jnp.sin(angles)
+    starts = sg[...].astype(f32)
+    column = jnp.broadcast_to(starts, (128, 1024)).T
+
+    @pl.loop(0, 8)
+    def _(i):
+        r = lanes(i * 128, 128)
+        here = jnp.broadcast_to(sg[:, r].astype(f32), (1024, 128))
+        big[:, r] = jnp.where(column == here, 0.0, neg_large)
+
+    diag(0)
+    done(0)
+    local(land.at[:, pl.ds(0, 128)], gains, "cg")
+    local(land.at[:, pl.ds(128, 384)], wq.at[0], "cq0")
+    diag(1)
+    shared_activation(xs, "ax")
+    arrived(gains, "cg")
+    gain_rows = gains[...].astype(f32).T
+    grow[...] = gain_rows[0:8]
+
+    @pl.loop(0, 4)
+    def _(i):
+        xb = xs[rows(i * 256, 256), :].astype(f32)
+        c = xb - jnp.mean(xb, -1, keepdims=True)
+        n = c * lax.rsqrt(jnp.mean(c * c, -1, keepdims=True) + norm_eps)
+        h1t[:, lanes(i * 256, 256)] = (n * grow[0:1, :]).astype(bf16).T
+
+    xystage(2)
+    xystage(3)
+    zstage(4)
+    zstage(5)
+    done(1)
+    local(land.at[:, pl.ds(512, 384)], wq.at[1], "cq1")
+    local(land.at[:, pl.ds(896, 384)], wq.at[2], "cq2")
+    for p in range(3):
+        arrived(wq.at[p], f"cq{p}")
+
+    @pl.loop(0, 3)
+    def _(p):
+        t = times(wq[p].T, h1t[...])
+        c = cosr[...]
+        s = sinr[...]
+        for hh in range(4):
+            u1 = t[hh * 64 : hh * 64 + 32]
+            u2 = t[hh * 64 + 32 : hh * 64 + 64]
+            scale = HEAD_DIM**-0.5 if hh < 2 else 1.0
+            qk[p, hh * 64 : hh * 64 + 32, :] = ((u1 * c - u2 * s) * scale).astype(bf16)
+            qk[p, hh * 64 + 32 : hh * 64 + 64, :] = ((u2 * c + u1 * s) * scale).astype(bf16)
+        qk[p, 256:384, :] = t[256:384].astype(bf16)
+
+    activation(dy_in, dys, "ay")
+
+    def weight_done(u):
+        done(u)
+        o, w = GATHER[u]
+        if u == 2:
+            pieces = [(land.at[:, pl.ds(o, w)], wa.at[k], None)]
+        elif u == 3:
+            pieces = [(land.at[:, pl.ds(o, w)], wi.at[k, :, pl.ds(0, 640)], None)]
+        elif u == 4:
+            pieces = [(land.at[:, pl.ds(o, w)], wi.at[k, :, pl.ds(640, 512)], None)]
+        else:
+            pieces = [
+                (land.at[:, pl.ds(o, 640)], wm.at[:, pl.ds(0, 640)], k == 0),
+                (land.at[:, pl.ds(o + 128, 512)], wm.at[:, pl.ds(640, 512)], k == 1),
+            ]
+        for src, dst, when in pieces:
+            if when is None:
+                local(src, dst, f"cw{u}")
+            else:
+                pl.when(when)(lambda src=src, dst=dst: local(src, dst, f"cw{u}") and None)
+            send(src, dst, f"pw{u}", (pn, z), when=when)
+
+    def weight_here(u):
+        if u == 2:
+            mine, theirs = [(wa.at[k], None)], [(wa.at[other], None)]
+        elif u == 3:
+            mine, theirs = [(wi.at[k, :, pl.ds(0, 640)], None)], [(wi.at[other, :, pl.ds(0, 640)], None)]
+        elif u == 4:
+            mine, theirs = [(wi.at[k, :, pl.ds(640, 512)], None)], [(wi.at[other, :, pl.ds(640, 512)], None)]
+        else:
+            low, high = wm.at[:, pl.ds(0, 640)], wm.at[:, pl.ds(640, 512)]
+            mine, theirs = [(low, k == 0), (high, k == 1)], [(low, k == 1), (high, k == 0)]
+        for group, name in ((mine, "cw"), (theirs, "pw")):
+            for ref, when in group:
+                if when is None:
+                    arrived(ref, f"{name}{u}")
+                else:
+                    pl.when(when)(lambda ref=ref, name=name: arrived(ref, f"{name}{u}"))
+
+    forward_steps = [
+        lambda: (diag(2), xystage(4)),
+        lambda: (diag(3), xystage(5)),
+        lambda: (weight_done(2), diag(4)),
+        lambda: (weight_done(3), diag(5)),
+        lambda: (weight_done(4), share_activation(dys, "ay")),
+        lambda: weight_done(5),
+    ]
+
+    for h in range(6):
+        p, hh, slot = h // 2, h % 2, h % 2
+        kt = qk[p, 128 + hh * 64 : 192 + hh * 64, :]
+        vt = qk[p, 256 + hh * 64 : 320 + hh * 64, :]
+        if h >= 2:
+            arrived(probs.at[slot], f"e{h - 2}")
+        orow = rows(k * 384 + h * 64, 64)
+
+        @pl.loop(0, 4)
+        def _(i):
+            cols = lanes(i * 256, 256)
+            s = dims(kt, qk[p, hh * 64 : hh * 64 + 64, cols], 0, 0) + big[:, cols]
+            e = jnp.exp(s - jnp.max(s, 0, keepdims=True))
+            r = 1.0 / jnp.sum(e, 0, keepdims=True)
+            eb = e.astype(bf16)
+            probs[slot, :, cols] = eb
+            otb[orow, cols] = (times(vt, eb) * r).astype(bf16)
+            rl[h : h + 1, cols] = r
+
+        local(probs.at[slot], keep.at[h], f"e{h}")
+        send(otb.at[orow, :], otb.at[orow, :], f"o{h}", (pn, z))
+        forward_steps[h]()
+
+    for u in range(2, 6):
+        weight_here(u)
+    for h in range(6):
+        arrived(otb.at[rows(other * 384 + h * 64, 64), :], f"o{h}")
+    arrived(probs.at[0], "e4")
+    arrived(probs.at[1], "e5")
+
+    mine = rows(k * 512, 512)
+    theirs = rows(other * 512, 512)
+    my_lanes = lanes(k * 512, 512)
+    ot_mine = otb[:, my_lanes]
+    x1[:, 0:384] = xs[mine, 0:384].astype(f32) + dims(ot_mine, wa[0], 0, 0)
+    x1[:, 384:768] = xs[mine, 384:768].astype(f32) + dims(ot_mine, wa[1], 0, 0)
+    xx = x1[...]
+    c = xx - jnp.mean(xx, -1, keepdims=True)
+    n = c * lax.rsqrt(jnp.mean(c * c, -1, keepdims=True) + norm_eps)
+    h2[mine, :] = (n * grow[1:2, :]).astype(bf16)
+    send(h2.at[mine, :], h2.at[mine, :], "h2", (pn, z))
+    for o, w in ((0, 512), (512, 512), (1024, 128)):
+        cols = pl.ds(o, w)
+        a = times(h2[mine, :], wi[0, :, cols])
+        b = times(h2[mine, :], wi[1, :, cols])
+        phi = 0.5 * (1.0 + lax.erf(a * 0.7071067811865476))
+        gelu = a * phi
+        hid[:, cols] = (gelu * b).astype(bf16)
+        big[0:512, cols] = b * (phi + a * (jnp.exp(-0.5 * a * a) * 0.3989422804014327))
+        big[512:1024, cols] = gelu
+    send(hid.at[:, lanes(other * 512, 640)], hidp, "hid", (pn, z))
+    lo[...] = (x1[...] + dims(hid[...], wm[...], 1, 1)).astype(bf16)
+    give_back(lo, lo_out, "alo")
+
+    for o, w in ((0, 512), (512, 512), (1024, 128)):
+        cols = pl.ds(o, w)
+        e = times(dys[mine, :], wm[:, cols])
+        dgo[0, :, cols] = (e * big[0:512, cols]).astype(bf16)
+        dgo[1, :, cols] = (e * big[512:1024, cols]).astype(bf16)
+    send(dgo.at[other], dgp, "dg", (pn, z))
+    f2 = dims(dgo[0], wi[0], 1, 1) + dims(dgo[1], wi[1], 1, 1)
+    xx = x1[...]
+    c = xx - jnp.mean(xx, -1, keepdims=True)
+    r2 = lax.rsqrt(jnp.mean(c * c, -1, keepdims=True) + norm_eps)
+    n = c * r2
+    grow[3:4, :] = jnp.sum(f2 * n, 0, keepdims=True)
+    cc = f2 * grow[1:2, :]
+    dx = dys[mine, :].astype(f32) + r2 * (
+        cc - jnp.mean(cc, -1, keepdims=True) - n * jnp.mean(cc * n, -1, keepdims=True)
+    )
+    x1[...] = dx
+    dx1b[...] = dx.astype(bf16)
+    send(dx1b.at[:, lanes(other * 384, 384)], dx1bp, "dx1b", (pn, z))
+    for part in range(2):
+        which = other if part == 0 else k
+        col = lanes(which * 384, 384)
+        feat = rows(which * 384, 384)
+        left = jnp.concatenate([wa[0, feat, :], wa[1, feat, :]], axis=1)
+        t = dims(left, dx1b[...], 1, 1).astype(bf16)
+        if part == 0:
+            dot_send[...] = t
+            send(dot_send, dot_own.at[:, my_lanes], "do", (pn, z))
+        else:
+            dot_own[:, my_lanes] = t
+    local(keep.at[5], probs.at[1], "b5")
+    local(keep.at[4], probs.at[0], "b4")
+
+    shared_activation(dys, "ay")
+    arrived(hidp, "hid")
+    grad[:, MLP : MLP + 640] = (
+        dims(dys[mine, :], hid[:, lanes(k * 512, 640)], 0, 0) + dims(dys[theirs, :], hidp[...], 0, 0)
+    ).astype(bf16)
+    s1("m")
+    arrived(h2.at[theirs, :], "h2")
+    arrived(dgp, "dg")
+    for name, o, w in (("i0", 0, 640), ("i1", 640, 512)):
+        cols = pl.ds(o, w)
+        grad[:, IN + o : IN + o + w] = (
+            dims(h2[mine, :], dgo[k, :, cols], 0, 0) + dims(h2[theirs, :], dgp[:, cols], 0, 0)
+        ).astype(bf16)
+        s1(name)
+    arrived(dx1bp, "dx1b")
+    grad[:, ATTN : ATTN + 384] = (
+        times(otb[:, my_lanes], dx1b[:, lanes(k * 384, 384)])
+        + times(otb[:, lanes(other * 512, 512)], dx1bp[...])
+    ).astype(bf16)
+    s1("a")
+    arrived(dot_own.at[:, lanes(other * 512, 512)], "do")
+
+    backward_steps = {
+        5: lambda: (s2("m"), s2("i0")),
+        4: lambda: (s3("m"), s2("i1")),
+        3: lambda: (s4("m"), s3("i0"), s2("a"), s2("q2")),
+        2: lambda: (s5("m"), s4("i0"), s3("i1"), s3("a")),
+        1: lambda: (s5("i0"), s4("i1"), s4("a"), s3("q2"), s2("q1")),
+        0: lambda: (s5("i1"), s5("a"), s4("q2"), s3("q1")),
+    }
+    for h in (5, 4, 3, 2, 1, 0):
+        p, hh, slot = h // 2, h % 2, h % 2
+        kt = qk[p, 128 + hh * 64 : 192 + hh * 64, :]
+        vt = qk[p, 256 + hh * 64 : 320 + hh * 64, :]
+        qr = slice(hh * 64, hh * 64 + 64)
+        arrived(probs.at[slot], f"b{h}")
+        dkb[...] = jnp.zeros_like(dkb)
+        dvb[...] = jnp.zeros_like(dvb)
+
+        @pl.loop(0, 4)
+        def _(i):
+            cols = lanes(i * 256, 256)
+            do = dot_own[h * 64 : h * 64 + 64, cols].astype(f32) * rl[h : h + 1, cols]
+            delta = jnp.sum(do * otb[rows(k * 384 + h * 64, 64), cols].astype(f32), 0, keepdims=True)
+            dob = do.astype(bf16)
+            e = probs[slot, :, cols]
+            ds = (e.astype(f32) * (dims(vt, dob, 0, 0) - delta)).astype(bf16)
+            dkb[...] += dims(qk[p, qr, cols], ds, 1, 1)
+            dvb[...] += dims(dob, e, 1, 1)
+            dq = times(kt, ds) * HEAD_DIM**-0.5
+            c = cosr[:, cols]
+            s = sinr[:, cols]
+            qk[p, hh * 64 : hh * 64 + 32, cols] = (dq[:32] * c + dq[32:] * s).astype(bf16)
+            qk[p, hh * 64 + 32 : hh * 64 + 64, cols] = (dq[32:] * c - dq[:32] * s).astype(bf16)
+
+        if h >= 2:
+            local(keep.at[h - 2], probs.at[slot], f"b{h - 2}")
+        d = dkb[...]
+        c = cosr[...]
+        s = sinr[...]
+        qk[p, 128 + hh * 64 : 160 + hh * 64, :] = (d[:32] * c + d[32:] * s).astype(bf16)
+        qk[p, 160 + hh * 64 : 192 + hh * 64, :] = (d[32:] * c - d[:32] * s).astype(bf16)
+        qk[p, 256 + hh * 64 : 320 + hh * 64, :] = dvb[...].astype(bf16)
+        if hh == 0:
+            grad[:, PAIR + 384 * p : PAIR + 384 * p + 384] = dims(h1t[...], qk[p], 1, 1).astype(bf16)
+            s1(f"q{p}")
+        backward_steps[h]()
+
+    def f1_part(cols):
+        return times(wq[0], qk[0, :, cols]) + times(wq[1], qk[1, :, cols]) + times(wq[2], qk[2, :, cols])
+
+    big[0:768, 0:512] = f1_part(lanes(other * 512, 512))
+    send(big.at[pl.ds(0, 768), pl.ds(0, 512)], f1r, "f1", (pn, z))
+    big[0:768, 512:1024] = f1_part(my_lanes)
+    s2("q0")
+    s5("q2")
+    s4("q1")
+    arrived(f1r, "f1")
+    f1 = (big[0:768, 512:1024] + f1r[...]).T
+    xx = xs[mine, :].astype(f32)
+    c = xx - jnp.mean(xx, -1, keepdims=True)
+    r1 = lax.rsqrt(jnp.mean(c * c, -1, keepdims=True) + norm_eps)
+    n = c * r1
+    grow[2:3, :] = jnp.sum(f1 * n, 0, keepdims=True)
+    cc = f1 * grow[0:1, :]
+    gi[...] = (
+        x1[...] + r1 * (cc - jnp.mean(cc, -1, keepdims=True) - n * jnp.mean(cc * n, -1, keepdims=True))
+    ).astype(bf16)
+    give_back(gi, gi_out, "agi")
+    two = jnp.concatenate([grow[2:4, :], jnp.zeros((126, 768), f32)], axis=0)
+    grad[:, 0:128] = two.T.astype(bf16)
+    s1("g")
+    s3("q0")
+    s5("q1")
+    s2("g")
+    s4("q0")
+    s3("g")
+    s5("q0")
+    s4("g")
+    s5("g")
+    for u in REDUCE:
+        s6(u)
+    given_back(lo_out, "alo")
+    given_back(gi_out, "agi")
+    for drain in drains:
+        drain()
+
+
+def pack(w_qkv, w_attn, w_in, w_mlp, g1, g2):
+    r = w_qkv.shape[0]
+    g = jnp.concatenate([g1[:, None], g2[:, None], jnp.zeros((r, 126), bf16)], axis=1)
+    g = jnp.broadcast_to(g[None], (2, r, 128))
+    qkv = w_qkv.reshape(r, 3, 2, 3, 128).transpose(2, 0, 3, 1, 4).reshape(2, r, 1152)
+    a = w_attn.reshape(r, 2, 384).transpose(1, 0, 2)
+    i = w_in.reshape(r, 2, 1152).transpose(1, 0, 2)
+    m = jnp.stack([w_mlp[:, :640], w_mlp[:, 512:]])
+    return jnp.concatenate([g, qkv, a, i, m], axis=2)
+
+
+def unpack(gp):
+    r = gp.shape[1]
+    gains = gp[0, :, 0:2] + gp[1, :, 0:2]
+    qkv = gp[:, :, 128:1280].reshape(2, r, 3, 3, 128).transpose(1, 3, 0, 2, 4).reshape(r, 2304)
+    a = gp[:, :, 1280:1664].transpose(1, 0, 2).reshape(r, 768)
+    i = gp[:, :, 1664:2816].transpose(1, 0, 2).reshape(r, 2304)
+    m = jnp.concatenate([gp[0, :, 2816:3456], gp[1, :, 2944:3456]], axis=1)
+    return qkv, a, i, m, gains[:, 0], gains[:, 1]
+
+
+def fast(layer_in, seg_start, out_grad, w_qkv, w_attn_out, w_in, w_mlp_out, norm_attn, norm_mlp):
+    wp = pack(w_qkv, w_attn_out, w_in, w_mlp_out, norm_attn, norm_mlp)
+    frequency = rope_base ** (-(jnp.arange(32).astype(f32) * 2.0) / HEAD_DIM)
+    freq = jnp.broadcast_to(frequency[:, None], (32, 128))
+    hbm = pl.BlockSpec(memory_space=pltpu.HBM)
+    vmem = pl.BlockSpec(memory_space=pltpu.VMEM)
+    V = pltpu.VMEM
+    outs = pl.pallas_call(
+        step_kernel,
+        name="layer",
+        out_shape=[
+            jax.ShapeDtypeStruct((2, 256, 768), bf16),
+            jax.ShapeDtypeStruct((2, 256, 768), bf16),
+            jax.ShapeDtypeStruct((2, 24, WIDTH), f32),
+            jax.ShapeDtypeStruct((768, WIDTH), bf16),
+            jax.ShapeDtypeStruct((6, 1024, 1024), bf16),
+        ],
+        in_specs=[hbm, hbm, hbm, vmem, vmem],
+        out_specs=[hbm] * 5,
+        scratch_shapes=[
+            V((1024, 768), bf16),
+            V((1024, 768), bf16),
+            V((1, 1024), jnp.int32),
+            V((768, 1024), bf16),
+            V((3, 768, 384), bf16),
+            V((2, 768, 384), bf16),
+            V((2, 768, 1152), bf16),
+            V((768, 1152), bf16),
+            V((768, 128), bf16),
+            V((32, 1024), f32),
+            V((32, 1024), f32),
+            V((3, 384, 1024), bf16),
+            V((1024, 1152), f32),
+            V((2, 1024, 1024), bf16),
+            V((768, 1024), bf16),
+            V((8, 1024), f32),
+            V((512, 768), f32),
+            V((1024, 768), bf16),
+            V((512, 1152), bf16),
+            V((512, 640), bf16),
+            V((2, 512, 1152), bf16),
+            V((512, 1152), bf16),
+            V((512, 768), bf16),
+            V((512, 384), bf16),
+            V((384, 512), bf16),
+            V((384, 1024), bf16),
+            V((768, 512), f32),
+            V((512, 768), bf16),
+            V((512, 768), bf16),
+            V((768, WIDTH), bf16),
+            V((8, 768), f32),
+            V((64, 1024), f32),
+            V((64, 1024), f32),
+            V((2, 96, WIDTH), bf16),
+            V((2, 96, WIDTH), bf16),
+            V((96, WIDTH), bf16),
+            V((96, WIDTH), bf16),
+            V((2, 4, 24, WIDTH), bf16),
+            V((2, 24, WIDTH), bf16),
+            V((2, 2, 24, WIDTH), bf16),
+            V((2, 24, WIDTH), bf16),
+            V((2, 24, WIDTH), f32),
+            pltpu.SemaphoreType.DMA((160,)),
+            pltpu.SemaphoreType.DMA((1,)),
+            pltpu.SemaphoreType.DMA((220,)),
+        ],
+        compiler_params=pltpu.CompilerParams(
+            collective_id=0, has_side_effects=True, vmem_limit_bytes=67043328
+        ),
+    )(layer_in, out_grad, seg_start[:, None, :], wp, freq)
+    return (outs[0], outs[1], *unpack(outs[2]))
 
 
 def normalize(values):
@@ -264,29 +949,14 @@
 
 
 def solution(mesh):
+    A = P(None, ("dp", "ctx"), None)
+    S = P(None, ("dp", "ctx"))
+    W = P(("dp", "ctx"), None)
+    G = P(("dp", "ctx"))
     return jax.shard_map(
-        local,
+        fast if dict(mesh.shape) == {"dp": 8, "ctx": 4} else local,
         mesh=mesh,
-        in_specs=(
-            P(None, ("dp", "ctx"), None),
-            P(None, ("dp", "ctx")),
-            P(None, ("dp", "ctx"), None),
-            P(("dp", "ctx"), None),
-            P(("dp", "ctx"), None),
-            P(("dp", "ctx"), None),
-            P(("dp", "ctx"), None),
-            P(("dp", "ctx")),
-            P(("dp", "ctx")),
-        ),
-        out_specs=(
-            P(None, ("dp", "ctx"), None),
-            P(None, ("dp", "ctx"), None),
-            P(("dp", "ctx"), None),
-            P(("dp", "ctx"), None),
-            P(("dp", "ctx"), None),
-            P(("dp", "ctx"), None),
-            P(("dp", "ctx")),
-            P(("dp", "ctx")),
-        ),
+        in_specs=(A, S, A, W, W, W, W, G, G),
+        out_specs=(A, A, W, W, W, W, G, G),
         check_vma=False,
     )

time: 1130 us -> 208 us (0.18)
  waiting for transfers between devices: 772 us -> 0 us
  Pallas kernels: 0 us -> 184 us
  matrix products: 124 us -> 0 us
  blocking collectives: 101 us -> 0 us
  other arithmetic: 50.2 us -> 2.1 us
  local copies, waits for them, and re-layouts: 57 us -> 20.3 us
  between operations: 15.5 us -> 0.69 us
    reduce_scatter x7 -> x0, waiting for transfers between devices: 380 us -> none  [the longest x1 125 us: local(): lax.psum_scatter(grad_sums[2], ('dp', 'ctx'), scatter_dimension=0, tiled=...]
    all_gather x8 -> x0, waiting for transfers between devices: 257 us -> none  [the longest x2 71.6 us: local(): lax.all_gather(keys_here, 'ctx', axis=0, tiled=True)]
    pallas_call x0 -> x1, Pallas kernels: none -> 184 us  [fast(): pl.pallas_call(step_kernel, name='layer', out_shape=[jax.ShapeDtypeStruct...]
    unnamed x17 -> x0, waiting for transfers between devices: 136 us -> none
    dot_general x66 -> x0, matrix products: 124 us -> none  [the longest x8 21.4 us: product(): return jnp.dot(left, right, preferred_element_type=jnp.float32)]
    unnamed x2 -> x0, blocking collectives: 82.5 us -> none
    convert_element_type x17 -> x0, other arithmetic: 19.8 us -> none  [the longest x6 7.83 us: attend_back(): grad_score = (attn_prob * (grad_prob - inner_sum)).astype(jnp.bfloat16)]
    all_gather x2 -> x0, blocking collectives: 18.5 us -> none  [local(): lax.all_gather(starts_here, 'ctx', axis=0, tiled=True)]
  transfers between devices with their start and end apart: 16 -> 0, of which waited for: 14 -> 0; matrix products, arithmetic and copies ran while one was open for 13% -> 0% of each run, Pallas kernels for 0% -> 0%
where the time goes in v1:
time: 208 us; the launch traced here: 207 us
  Pallas kernels  184 us (88%)
  local copies, waits for them, and re-layouts  20.3 us (10%)
  other arithmetic  2.1 us (1%)
    pallas_call x1, Pallas kernels, fast(): pl.pallas_call(step_kernel, name='layer', out_shape=[jax.ShapeDtypeStruct...  184 us
    unnamed x8, local copies, waits for them, and re-layouts  10.3 us

profile of v1, /device:TPU:0, one launch (start us, length us, event | category | flops | bytes accessed | tf_op | source)
XLA Modules:
  0.0 207.1 jit_solution(9142876752954052670)
XLA Ops:
  0.6 0.1 pad.6.clone
  0.7 1.3 broadcast_in_dim.24.seg_in
  2.0 0.7 copy.22
  2.7 0.7 copy.23
  3.5 0.1 maximum_maximum_fusion
  3.6 0.7 broadcast_in_dim.29.freq
  4.2 0.8 slice_bitcast_fusion.5
  5.1 0.9 reshape.50
  6.0 0.1 copy.24
  6.1 0.1 reshape.51
  6.2 0.6 constant_dynamic-update-slice_fusion.1
  6.8 0.7 constant_dynamic-update-slice_fusion
  7.5 1.4 fusion.1
  8.8 1.5 fusion
  10.4 0.6 maximum_dynamic-update-slice_fusion.wp
  11.0 184.1 %layer.1 = (bf16[2,256,768]{2,1,0:T(8,128)(2,1)}, bf16[2,256,768]{2,1,0:T(8,128)(2,1)}, f32[2,24,3456]{2,1,0:T(8,128)}, bf16[768,3456]{1,0:T(8,128)(2,1)}, bf16[6,1024,1024]{2,1,0:T(8,128)(2,1)}) custom-call(bf16[2,256,768]{2,1,0:T(8,128)(2,1)} %x_in.1, bf16[2,256,768]{2,1,0:T(8,128)(2,1)} %dy_in.1, s32[2,1,256]{2,1,0:T(1,128)} %broadcast_in_dim.24.seg_in, ...), custom_call_target="tpu_custom_call" | custom-call | tf_op jit(solution)/shard_map/layer/pallas_call | solution.py:635
  195.1 0.7 slice_add_fusion
  195.8 0.1 copy.30
  195.9 0.5 slice_bitcast_fusion.6
  196.4 0.8 slice_bitcast_fusion.3
  197.3 0.8 slice_bitcast_fusion.2
  198.1 0.7 pad_maximum_fusion
  198.7 0.9 slice_bitcast_fusion.1
  199.6 1.1 slice_bitcast_fusion
  200.7 0.7 copy.34
  201.4 0.6 copy.33
  202.0 0.1 reshape.54
  202.1 0.1 copy.27
  202.2 0.8 reshape.55
  203.0 2.1 copy.43
  205.1 2.1 copy.44
  (2 shorter events, 0.0 us)

commit v2 on v1

--- a/solution.py
+++ b/solution.py
@@ -1,6 +1,8 @@
-import functools
+import contextlib
+
 import jax
 import jax.numpy as jnp
+import numpy as np
 from jax import lax
 from jax.experimental import pallas as pl
 from jax.experimental.pallas import tpu as pltpu
@@ -35,6 +37,21 @@
 }
 
 
+TRACE = False
+
+
+def scope(name):
+    return jax.named_scope(name) if TRACE else contextlib.nullcontext()
+
+
+def scoped(fn):
+    def inner(*args):
+        with scope(f"{fn.__name__}_{args[0] if args and isinstance(args[0], (int, str)) else ''}"):
+            return fn(*args)
+
+    return inner
+
+
 def dims(left, right, left_at, right_at):
     return lax.dot_general(
         left, right, (((left_at,), (right_at,)), ((), ())), preferred_element_type=f32
@@ -46,8 +63,9 @@
 
 
 def step_kernel(
-    x_in, dy_in, seg_in, wp, freq,
+    x_in, dy_in, seg_in, w_qkv, w_attn, w_in, w_mlp, g_attn, g_mlp, freq,
     lo_out, gi_out, gp_out, land, keep,
+    wp, gcol,
     xs, dys, sg, h1t, wq, wa, wi, wm, gains, cosr, sinr, qk, big, probs, otb, rl, x1, h2, hid, hidp,
     dgo, dgp, dx1b, dx1bp, dot_send, dot_own, f1r, lo, gi, grad, grow, dkb, dvb,
     ra, rb, ra2, rb2, zs, zp, zm, zx, fin,
@@ -76,19 +94,34 @@
     def rsem(name):
         return rs_.at[names.setdefault(name, len(names))]
 
-    def send(src, dst, name, dev, when=None):
+    def still(view):
+        index = view.transforms[0].indices
+        return view.ref.at[tuple(pl.ds(0, at.size) if hasattr(at, "size") else 0 for at in index)]
+
+    def send(src, dst, name, dev, when=None, sem=None):
         i = count["send"]
         count["send"] += 1
         copy = pltpu.make_async_remote_copy(
-            src_ref=src, dst_ref=dst, send_sem=sends.at[i], recv_sem=rsem(name),
+            src_ref=src, dst_ref=dst, send_sem=sends.at[i], recv_sem=rsem(name) if sem is None else sem,
             device_id=dev, device_id_type=MESH,
         )
         if when is None:
             copy.start()
-            drains.append(copy.wait_send)
         else:
-            pl.when(when)(copy.start)
-            drains.append(lambda: pl.when(when)(copy.wait_send))
+            pl.when(when())(copy.start)
+        drains.append((i, src, when))
+
+    def drain_all():
+        for i, src, when in drains:
+            view = still(src) if hasattr(src, "transforms") else src
+
+            def wait(view=view, i=i):
+                pltpu.make_async_copy(view, view, sends.at[i]).wait()
+
+            if when is None:
+                wait()
+            else:
+                pl.when(when())(wait)
 
     def local(src, dst, name):
         copy = pltpu.make_async_copy(src, dst, rsem(name))
@@ -112,8 +145,29 @@
             )
     for dev in (pn, xn, yn):
         pl.semaphore_signal(barrier, inc=1, device_id=(dev, z), device_id_type=MESH)
-    pl.semaphore_wait(barrier, 9)
-
+
+    packs = []
+    for c in range(2):
+        for p in range(3):
+            for t in range(3):
+                packs.append((w_qkv, 768 * t + 384 * c + 128 * p, c, PAIR + 384 * p + 128 * t, 128))
+        packs.append((w_attn, 384 * c, c, ATTN, 384))
+        packs.append((w_in, 1152 * c, c, IN, 1152))
+        packs.append((w_mlp, 512 * c, c, MLP, 640))
+    packing = [
+        pltpu.make_async_copy(w.at[:, pl.ds(o, n)], wp.at[c, :, pl.ds(at, n)], ls_.at[i])
+        for i, (w, o, c, at, n) in enumerate(packs)
+    ]
+    for copy in packing:
+        copy.start()
+    gcol[...] = jnp.zeros_like(gcol)
+    gcol[0:1, 0:24] = g_attn[...].astype(f32)
+    gcol[1:2, 0:24] = g_mlp[...].astype(f32)
+    columns = jnp.concatenate([gcol[...], jnp.zeros((120, 128), f32)], axis=0).T[0:24].astype(bf16)
+    wp[0, :, 0:128] = columns
+    wp[1, :, 0:128] = columns
+
+    @scoped
     def zstage(u):
         o, w = GATHER[u]
         cols = pl.ds(o, w)
@@ -122,9 +176,10 @@
             src = wp.at[c, :, cols]
             send(src, dst, f"z{u}", (2 * q + c, zn))
             send(src, dst, f"z{u}", (2 * q + c, zb))
-            send(src, dst, f"z{u}", (pn, z), when=k != c)
+            send(src, dst, f"z{u}", (pn, z), when=lambda c=c: k != c)
             pl.when(k == c)(lambda src=src: local(src, dst, f"z{u}") and None)
 
+    @scoped
     def xystage(u):
         o, w = GATHER[u]
         cols = pl.ds(o, w)
@@ -134,8 +189,9 @@
         send(slab, slab, f"y{u}", (yn, z))
         for j in range(2):
             part = land.at[rows((2 * q + j) * 96 + lax.rem(4 - 2 * z + 4, 4) * 24, 48), cols]
-            send(part, part, f"z{u}", (dp, zn), when=inner)
-
+            send(part, part, f"z{u}", (dp, zn), when=lambda: inner)
+
+    @scoped
     def diag(u):
         o, w = GATHER[u]
         cols = pl.ds(o, w)
@@ -146,27 +202,28 @@
         part = land.at[rows(qy * 192 + 96, 96), cols]
         send(part, part, f"dy{u}", (xn, z))
 
+    @scoped
     def done(u):
         o, w = GATHER[u]
         cols = pl.ds(o, w)
         arrived(land.at[rows(qd * 192, 96), cols], f"dx{u}")
         arrived(land.at[rows(qd * 192 + 96, 96), cols], f"dy{u}")
 
-    def activation(src_ref, dst_ref, name):
+    def activation(src_ref, dst_ref, name, turn=None):
         for m in range(2):
-            to = 2 * k + m
             src = src_ref.at[m]
             dst = dst_ref.at[rows(z * 256, 256), :]
             sem = rs_.at[base[name] + lax.rem(z, 2)]
-            i = count["send"]
-            count["send"] += 1
-            copy = pltpu.make_async_remote_copy(
-                src_ref=src, dst_ref=dst, send_sem=sends.at[i], recv_sem=sem,
-                device_id=(2 * q + zh, to), device_id_type=MESH,
-            )
-            pl.when(to != z)(copy.start)
-            pl.when(to == z)(pltpu.make_async_copy(src, dst, sem).start)
-            drains.append(lambda copy=copy, to=to: pl.when(to != z)(copy.wait_send))
+
+            def away(m=m):
+                there = 2 * k + m != z
+                return there if turn is None else jnp.logical_and(turn, there)
+
+            here = 2 * k + m == z
+            if turn is not None:
+                here = jnp.logical_and(turn, here)
+            send(src, dst, None, (2 * q + zh, 2 * k + m), when=away, sem=sem)
+            pl.when(here)(pltpu.make_async_copy(src, dst, sem).start)
 
     base = {}
     for name in ("ax", "ay", "alo", "agi"):
@@ -174,57 +231,50 @@
         names[name + "0"] = len(names)
         names[name + "1"] = len(names)
 
+    @scoped
     def share_activation(ref, name):
         for j in range(2):
             r = rows(k * 512 + j * 256, 256)
             arrived(ref.at[r, :], f"{name}{j}")
             send(ref.at[r, :], ref.at[r, :], f"p{name}{j}", (pn, z))
 
+    @scoped
     def shared_activation(ref, name):
         for j in range(2):
             arrived(ref.at[rows(other * 512 + j * 256, 256), :], f"p{name}{j}")
 
-    def give_back(src_ref, out_ref, name):
+    @scoped
+    def give_back(src_ref, out_ref, name, blocks=(0, 1)):
         m = lax.rem(z, 2)
-        for j in range(2):
-            to = 2 * k + j
+        for j in blocks:
             src = src_ref.at[pl.ds(j * 256, 256), :]
             dst = out_ref.at[m]
             sem = rs_.at[base[name] + m]
-            i = count["send"]
-            count["send"] += 1
-            copy = pltpu.make_async_remote_copy(
-                src_ref=src, dst_ref=dst, send_sem=sends.at[i], recv_sem=sem,
-                device_id=(2 * q + zh, to), device_id_type=MESH,
-            )
-            here = jnp.logical_and(to == z, zh == k)
-            away = jnp.logical_not(here)
-            pl.when(away)(copy.start)
-            pl.when(here)(pltpu.make_async_copy(src, dst, sem).start)
-            drains.append(lambda copy=copy, away=away: pl.when(away)(copy.wait_send))
-
+
+            def away(j=j):
+                return jnp.logical_or(2 * k + j != z, zh != k)
+
+            send(src, dst, None, (2 * q + zh, 2 * k + j), when=away, sem=sem)
+            pl.when(jnp.logical_not(away()))(pltpu.make_async_copy(src, dst, sem).start)
+
+    @scoped
     def given_back(out_ref, name):
         for m in range(2):
             arrived(out_ref.at[m], f"{name}{m}")
 
     def seg_send():
         for m in range(2):
-            to = 2 * k + m
-            src = seg_in.at[m]
+            src = seg_in.at[pl.ds(m, 1), :]
             dst = sg.at[:, lanes(z * 256, 256)]
             for c in range(2):
-                i = count["send"]
-                count["send"] += 1
-                copy = pltpu.make_async_remote_copy(
-                    src_ref=src, dst_ref=dst, send_sem=sends.at[i], recv_sem=rsem("seg"),
-                    device_id=(2 * q + c, to), device_id_type=MESH,
-                )
-                here = jnp.logical_and(to == z, k == c)
-                away = jnp.logical_not(here)
-                pl.when(away)(copy.start)
-                pl.when(here)(pltpu.make_async_copy(src, dst, rsem("seg")).start)
-                drains.append(lambda copy=copy, away=away: pl.when(away)(copy.wait_send))
-
+
+                def away(m=m, c=c):
+                    return jnp.logical_or(2 * k + m != z, k != c)
+
+                send(src, dst, "seg", (2 * q + c, 2 * k + m), when=away)
+                pl.when(jnp.logical_not(away()))(pltpu.make_async_copy(src, dst, rsem("seg")).start)
+
+    @scoped
     def s1(u):
         o, w = REDUCE[u]
         cols = pl.ds(o, w)
@@ -233,6 +283,7 @@
         for slot, quarter in enumerate((qy, qd)):
             send(grad.at[rows(quarter * 192 + 96, 96), cols], rb.at[slot, :, cols], f"rb{u}", (yn, z))
 
+    @scoped
     def s2(u):
         o, w = REDUCE[u]
         cols = pl.ds(o, w)
@@ -245,6 +296,7 @@
         grad[r2, cols] = (grad[r2, cols].astype(f32) + rb[1, :, cols].astype(f32)).astype(bf16)
         send(grad.at[r2, cols], rb2.at[:, cols], f"rb2{u}", (xn, z))
 
+    @scoped
     def s3(u):
         o, w = REDUCE[u]
         cols = pl.ds(o, w)
@@ -260,8 +312,9 @@
                 zs[j, at, :, cols] = total[24 * at : 24 * at + 24].astype(bf16)
         send(zs.at[:, zn, :, cols], zp.at[:, :, cols], f"zp{u}", (dp, zn))
         far = 2 * (1 - zh)
-        send(zs.at[:, pl.ds(far, 2), :, cols], zm.at[:, :, :, cols], f"zm{u}", (dp, zn), when=outer)
-
+        send(zs.at[:, pl.ds(far, 2), :, cols], zm.at[:, :, :, cols], f"zm{u}", (dp, zn), when=lambda: outer)
+
+    @scoped
     def s4(u):
         o, w = REDUCE[u]
         cols = pl.ds(o, w)
@@ -277,8 +330,9 @@
                     ).astype(bf16)
 
         for at in range(2):
-            send(zs.at[:, far + at, :, cols], zx.at[:, :, cols], f"zx{u}", (dp, far + at), when=inner)
-
+            send(zs.at[:, far + at, :, cols], zx.at[:, :, cols], f"zx{u}", (dp, far + at), when=lambda: inner)
+
+    @scoped
     def s5(u):
         o, w = REDUCE[u]
         cols = pl.ds(o, w)
@@ -291,21 +345,25 @@
         local(fin.at[k, :, cols], gp_out.at[k, :, cols], f"fl{u}")
         send(fin.at[other, :, cols], gp_out.at[k, :, cols], f"fr{u}", (pn, z))
 
+    @scoped
     def s6(u):
         o, w = REDUCE[u]
         cols = pl.ds(o, w)
         arrived(gp_out.at[k, :, cols], f"fl{u}")
         arrived(gp_out.at[other, :, cols], f"fr{u}")
 
-    zstage(0)
-    activation(x_in, xs, "ax")
+    pl.semaphore_wait(barrier, 9)
+
+    for copy in packing:
+        copy.wait()
+    for u in range(6):
+        zstage(u)
     seg_send()
-    zstage(1)
+    activation(x_in, xs, "ax", outer)
     xystage(0)
-    share_activation(xs, "ax")
     xystage(1)
-    zstage(2)
-    zstage(3)
+    xystage(2)
+    activation(x_in, xs, "ax", inner)
     arrived(sg, "seg")
     positions = (lax.broadcasted_iota(jnp.int32, (1, 1024), 1) - sg[...]).astype(f32)
     angles = freq[:, 0:1] * positions
@@ -321,26 +379,26 @@
         big[:, r] = jnp.where(column == here, 0.0, neg_large)
 
     diag(0)
+    xystage(3)
+    diag(1)
+    xystage(4)
+    share_activation(xs, "ax")
     done(0)
     local(land.at[:, pl.ds(0, 128)], gains, "cg")
     local(land.at[:, pl.ds(128, 384)], wq.at[0], "cq0")
-    diag(1)
-    shared_activation(xs, "ax")
     arrived(gains, "cg")
     gain_rows = gains[...].astype(f32).T
     grow[...] = gain_rows[0:8]
-
-    @pl.loop(0, 4)
-    def _(i):
-        xb = xs[rows(i * 256, 256), :].astype(f32)
-        c = xb - jnp.mean(xb, -1, keepdims=True)
-        n = c * lax.rsqrt(jnp.mean(c * c, -1, keepdims=True) + norm_eps)
-        h1t[:, lanes(i * 256, 256)] = (n * grow[0:1, :]).astype(bf16).T
-
-    xystage(2)
-    xystage(3)
-    zstage(4)
-    zstage(5)
+    shared_activation(xs, "ax")
+
+    with scope("ln1"):
+        @pl.loop(0, 4)
+        def _(i):
+            xb = xs[rows(i * 256, 256), :].astype(f32)
+            c = xb - jnp.mean(xb, -1, keepdims=True)
+            n = c * lax.rsqrt(jnp.mean(c * c, -1, keepdims=True) + norm_eps)
+            h1t[:, lanes(i * 256, 256)] = (n * grow[0:1, :]).astype(bf16).T
+
     done(1)
     local(land.at[:, pl.ds(512, 384)], wq.at[1], "cq1")
     local(land.at[:, pl.ds(896, 384)], wq.at[2], "cq2")
@@ -360,8 +418,14 @@
             qk[p, hh * 64 + 32 : hh * 64 + 64, :] = ((u2 * c + u1 * s) * scale).astype(bf16)
         qk[p, 256:384, :] = t[256:384].astype(bf16)
 
-    activation(dy_in, dys, "ay")
-
+        @pl.when(p == 1)
+        def _():
+            xystage(5)
+            activation(dy_in, dys, "ay")
+            diag(2)
+            diag(3)
+
+    @scoped
     def weight_done(u):
         done(u)
         o, w = GATHER[u]
@@ -373,16 +437,17 @@
             pieces = [(land.at[:, pl.ds(o, w)], wi.at[k, :, pl.ds(640, 512)], None)]
         else:
             pieces = [
-                (land.at[:, pl.ds(o, 640)], wm.at[:, pl.ds(0, 640)], k == 0),
-                (land.at[:, pl.ds(o + 128, 512)], wm.at[:, pl.ds(640, 512)], k == 1),
+                (land.at[:, pl.ds(o, 640)], wm.at[:, pl.ds(0, 640)], lambda: k == 0),
+                (land.at[:, pl.ds(o + 128, 512)], wm.at[:, pl.ds(640, 512)], lambda: k == 1),
             ]
         for src, dst, when in pieces:
             if when is None:
                 local(src, dst, f"cw{u}")
             else:
-                pl.when(when)(lambda src=src, dst=dst: local(src, dst, f"cw{u}") and None)
+                pl.when(when())(lambda src=src, dst=dst: local(src, dst, f"cw{u}") and None)
             send(src, dst, f"pw{u}", (pn, z), when=when)
 
+    @scoped
     def weight_here(u):
         if u == 2:
             mine, theirs = [(wa.at[k], None)], [(wa.at[other], None)]
@@ -400,37 +465,46 @@
                 else:
                     pl.when(when)(lambda ref=ref, name=name: arrived(ref, f"{name}{u}"))
 
-    forward_steps = [
-        lambda: (diag(2), xystage(4)),
-        lambda: (diag(3), xystage(5)),
-        lambda: (weight_done(2), diag(4)),
-        lambda: (weight_done(3), diag(5)),
-        lambda: (weight_done(4), share_activation(dys, "ay")),
-        lambda: weight_done(5),
-    ]
-
     for h in range(6):
-        p, hh, slot = h // 2, h % 2, h % 2
-        kt = qk[p, 128 + hh * 64 : 192 + hh * 64, :]
-        vt = qk[p, 256 + hh * 64 : 320 + hh * 64, :]
-        if h >= 2:
-            arrived(probs.at[slot], f"e{h - 2}")
+        rsem(f"e{h}")
+        rsem(f"o{h}")
+    first_send = count["send"]
+    count["send"] += 6
+    forward_steps = {
+        0: lambda: diag(4),
+        1: lambda: (weight_done(2), diag(5)),
+        2: lambda: weight_done(3),
+        3: lambda: weight_done(4),
+        4: lambda: weight_done(5),
+    }
+
+    @pl.loop(0, 6)
+    def _(h):
+        p, hh = h // 2, lax.rem(h, 2)
+        qrow, krow, vrow = (rows(at + hh * 64, 64) for at in (0, 128, 256))
         orow = rows(k * 384 + h * 64, 64)
 
-        @pl.loop(0, 4)
-        def _(i):
-            cols = lanes(i * 256, 256)
-            s = dims(kt, qk[p, hh * 64 : hh * 64 + 64, cols], 0, 0) + big[:, cols]
-            e = jnp.exp(s - jnp.max(s, 0, keepdims=True))
-            r = 1.0 / jnp.sum(e, 0, keepdims=True)
-            eb = e.astype(bf16)
-            probs[slot, :, cols] = eb
-            otb[orow, cols] = (times(vt, eb) * r).astype(bf16)
-            rl[h : h + 1, cols] = r
-
-        local(probs.at[slot], keep.at[h], f"e{h}")
-        send(otb.at[orow, :], otb.at[orow, :], f"o{h}", (pn, z))
-        forward_steps[h]()
+        @pl.when(h >= 2)
+        def _():
+            pltpu.make_async_copy(probs.at[hh], keep.at[h - 2], rs_.at[names["e0"] + 2 * (h - 2)]).wait()
+
+        s = dims(qk[p, krow, :], qk[p, qrow, :], 0, 0) + big[:, 0:1024]
+        e = jnp.exp(s - jnp.max(s, 0, keepdims=True))
+        r = 1.0 / jnp.sum(e, 0, keepdims=True)
+        eb = e.astype(bf16)
+        probs[hh] = eb
+        otb[orow, :] = (times(qk[p, vrow, :], eb) * r).astype(bf16)
+        rl[pl.ds(h, 1), :] = r
+        pltpu.make_async_copy(probs.at[hh], keep.at[h], rs_.at[names["e0"] + 2 * h]).start()
+        pltpu.make_async_remote_copy(
+            src_ref=otb.at[orow, :], dst_ref=otb.at[orow, :], send_sem=sends.at[first_send + h],
+            recv_sem=rs_.at[names["o0"] + 2 * h], device_id=(pn, z), device_id_type=MESH,
+        ).start()
+        for at, step in forward_steps.items():
+            pl.when(h == at)(lambda step=step: step() and None)
+
+    for h in range(6):
+        drains.append((first_send + h, otb.at[pl.ds(0, 64), :], None))
 
     for u in range(2, 6):
         weight_here(u)
@@ -463,6 +537,13 @@
     lo[...] = (x1[...] + dims(hid[...], wm[...], 1, 1)).astype(bf16)
     give_back(lo, lo_out, "alo")
 
+    share_activation(dys, "ay")
+    shared_activation(dys, "ay")
+    arrived(hidp, "hid")
+    grad[:, MLP : MLP + 640] = (
+        dims(dys[mine, :], hid[:, lanes(k * 512, 640)], 0, 0) + dims(dys[theirs, :], hidp[...], 0, 0)
+    ).astype(bf16)
+    s1("m")
     for o, w in ((0, 512), (512, 512), (1024, 128)):
         cols = pl.ds(o, w)
         e = times(dys[mine, :], wm[:, cols])
@@ -493,15 +574,10 @@
             send(dot_send, dot_own.at[:, my_lanes], "do", (pn, z))
         else:
             dot_own[:, my_lanes] = t
-    local(keep.at[5], probs.at[1], "b5")
-    local(keep.at[4], probs.at[0], "b4")
-
-    shared_activation(dys, "ay")
-    arrived(hidp, "hid")
-    grad[:, MLP : MLP + 640] = (
-        dims(dys[mine, :], hid[:, lanes(k * 512, 640)], 0, 0) + dims(dys[theirs, :], hidp[...], 0, 0)
-    ).astype(bf16)
-    s1("m")
+    local(keep.at[5], probs.at[1], "e5")
+    local(keep.at[4], probs.at[0], "e4")
+
+    s2("m")
     arrived(h2.at[theirs, :], "h2")
     arrived(dgp, "dg")
     for name, o, w in (("i0", 0, 640), ("i1", 640, 512)):
@@ -518,61 +594,76 @@
     s1("a")
     arrived(dot_own.at[:, lanes(other * 512, 512)], "do")
 
+    for h in range(6):
+        rsem(f"b{h}")
     backward_steps = {
-        5: lambda: (s2("m"), s2("i0")),
-        4: lambda: (s3("m"), s2("i1")),
-        3: lambda: (s4("m"), s3("i0"), s2("a"), s2("q2")),
-        2: lambda: (s5("m"), s4("i0"), s3("i1"), s3("a")),
-        1: lambda: (s5("i0"), s4("i1"), s4("a"), s3("q2"), s2("q1")),
-        0: lambda: (s5("i1"), s5("a"), s4("q2"), s3("q1")),
+        5: lambda: s3("m"),
+        4: lambda: (s1("q2"), s2("i0")),
+        3: lambda: (s2("i1"), s4("m")),
+        2: lambda: (s1("q1"), s2("a"), s5("m"), s3("i0")),
+        1: lambda: s2("q2"),
+        0: lambda: (s1("q0"), s4("i0"), s3("i1"), s3("a")),
     }
-    for h in (5, 4, 3, 2, 1, 0):
-        p, hh, slot = h // 2, h % 2, h % 2
-        kt = qk[p, 128 + hh * 64 : 192 + hh * 64, :]
-        vt = qk[p, 256 + hh * 64 : 320 + hh * 64, :]
-        qr = slice(hh * 64, hh * 64 + 64)
-        arrived(probs.at[slot], f"b{h}")
-        dkb[...] = jnp.zeros_like(dkb)
-        dvb[...] = jnp.zeros_like(dvb)
-
-        @pl.loop(0, 4)
-        def _(i):
-            cols = lanes(i * 256, 256)
-            do = dot_own[h * 64 : h * 64 + 64, cols].astype(f32) * rl[h : h + 1, cols]
+
+    @pl.loop(0, 6)
+    def _(turn):
+        h = 5 - turn
+        p, hh = h // 2, lax.rem(h, 2)
+        qrow, krow, vrow = (rows(at + hh * 64, 64) for at in (0, 128, 256))
+        arrived_at = rs_.at[names["e0"] + 2 * h]
+        pltpu.make_async_copy(keep.at[h], probs.at[hh], arrived_at).wait()
+        vt = qk[p, vrow, :]
+        kt = qk[p, krow, :]
+        for i in range(2):
+            cols = slice(i * 512, i * 512 + 512)
+            do = dot_own[rows(h * 64, 64), cols].astype(f32) * rl[pl.ds(h, 1), cols]
             delta = jnp.sum(do * otb[rows(k * 384 + h * 64, 64), cols].astype(f32), 0, keepdims=True)
             dob = do.astype(bf16)
-            e = probs[slot, :, cols]
+            e = probs[hh, :, cols]
             ds = (e.astype(f32) * (dims(vt, dob, 0, 0) - delta)).astype(bf16)
-            dkb[...] += dims(qk[p, qr, cols], ds, 1, 1)
-            dvb[...] += dims(dob, e, 1, 1)
+            dk = dims(qk[p, qrow, cols], ds, 1, 1)
+            dv = dims(dob, e, 1, 1)
+            if i == 0:
+                dkb[...] = dk
+                dvb[...] = dv
+            else:
+                dkb[...] += dk
+                dvb[...] += dv
             dq = times(kt, ds) * HEAD_DIM**-0.5
             c = cosr[:, cols]
             s = sinr[:, cols]
-            qk[p, hh * 64 : hh * 64 + 32, cols] = (dq[:32] * c + dq[32:] * s).astype(bf16)
-            qk[p, hh * 64 + 32 : hh * 64 + 64, cols] = (dq[32:] * c - dq[:32] * s).astype(bf16)
-
-        if h >= 2:
-            local(keep.at[h - 2], probs.at[slot], f"b{h - 2}")
+            qk[p, rows(hh * 64, 32), cols] = (dq[:32] * c + dq[32:] * s).astype(bf16)
+            qk[p, rows(hh * 64 + 32, 32), cols] = (dq[32:] * c - dq[:32] * s).astype(bf16)
+
+        @pl.when(h >= 2)
+        def _():
+            pltpu.make_async_copy(keep.at[h - 2], probs.at[hh], rs_.at[names["e0"] + 2 * (h - 2)]).start()
+
         d = dkb[...]
         c = cosr[...]
         s = sinr[...]
-        qk[p, 128 + hh * 64 : 160 + hh * 64, :] = (d[:32] * c + d[32:] * s).astype(bf16)
-        qk[p, 160 + hh * 64 : 192 + hh * 64, :] = (d[32:] * c - d[:32] * s).astype(bf16)
-        qk[p, 256 + hh * 64 : 320 + hh * 64, :] = dvb[...].astype(bf16)
-        if hh == 0:
-            grad[:, PAIR + 384 * p : PAIR + 384 * p + 384] = dims(h1t[...], qk[p], 1, 1).astype(bf16)
-            s1(f"q{p}")
-        backward_steps[h]()
+        qk[p, rows(128 + hh * 64, 32), :] = (d[:32] * c + d[32:] * s).astype(bf16)
+        qk[p, rows(160 + hh * 64, 32), :] = (d[32:] * c - d[:32] * s).astype(bf16)
+        qk[p, vrow, :] = dvb[...].astype(bf16)
+
+        @pl.when(hh == 0)
+        def _():
+            grad[:, lanes(PAIR + 384 * p, 384)] = dims(h1t[...], qk[p], 1, 1).astype(bf16)
+
+        for at, step in backward_steps.items():
+            pl.when(h == at)(lambda step=step: step() and None)
 
     def f1_part(cols):
         return times(wq[0], qk[0, :, cols]) + times(wq[1], qk[1, :, cols]) + times(wq[2], qk[2, :, cols])
 
     big[0:768, 0:512] = f1_part(lanes(other * 512, 512))
     send(big.at[pl.ds(0, 768), pl.ds(0, 512)], f1r, "f1", (pn, z))
+    s4("i1")
     big[0:768, 512:1024] = f1_part(my_lanes)
-    s2("q0")
-    s5("q2")
-    s4("q1")
+    s3("q2")
+    s2("q1")
+    s5("i0")
+    s4("a")
     arrived(f1r, "f1")
     f1 = (big[0:768, 512:1024] + f1r[...]).T
     xx = xs[mine, :].astype(f32)
@@ -584,51 +675,65 @@
     gi[...] = (
         x1[...] + r1 * (cc - jnp.mean(cc, -1, keepdims=True) - n * jnp.mean(cc * n, -1, keepdims=True))
     ).astype(bf16)
-    give_back(gi, gi_out, "agi")
     two = jnp.concatenate([grow[2:4, :], jnp.zeros((126, 768), f32)], axis=0)
     grad[:, 0:128] = two.T.astype(bf16)
     s1("g")
+    give_back(gi, gi_out, "agi", (0,))
+    s4("q2")
+    s2("q0")
+    s3("q1")
+    s5("i1")
+    s5("a")
+    give_back(gi, gi_out, "agi", (1,))
+    s2("g")
     s3("q0")
+    s4("q1")
+    s3("g")
+    s5("q2")
+    s4("q0")
+    s4("g")
     s5("q1")
-    s2("g")
-    s4("q0")
-    s3("g")
     s5("q0")
-    s4("g")
     s5("g")
     for u in REDUCE:
         s6(u)
     given_back(lo_out, "alo")
     given_back(gi_out, "agi")
-    for drain in drains:
-        drain()
-
-
-def pack(w_qkv, w_attn, w_in, w_mlp, g1, g2):
-    r = w_qkv.shape[0]
-    g = jnp.concatenate([g1[:, None], g2[:, None], jnp.zeros((r, 126), bf16)], axis=1)
-    g = jnp.broadcast_to(g[None], (2, r, 128))
-    qkv = w_qkv.reshape(r, 3, 2, 3, 128).transpose(2, 0, 3, 1, 4).reshape(2, r, 1152)
-    a = w_attn.reshape(r, 2, 384).transpose(1, 0, 2)
-    i = w_in.reshape(r, 2, 1152).transpose(1, 0, 2)
-    m = jnp.stack([w_mlp[:, :640], w_mlp[:, 512:]])
-    return jnp.concatenate([g, qkv, a, i, m], axis=2)
-
-
-def unpack(gp):
-    r = gp.shape[1]
-    gains = gp[0, :, 0:2] + gp[1, :, 0:2]
-    qkv = gp[:, :, 128:1280].reshape(2, r, 3, 3, 128).transpose(1, 3, 0, 2, 4).reshape(r, 2304)
-    a = gp[:, :, 1280:1664].transpose(1, 0, 2).reshape(r, 768)
-    i = gp[:, :, 1664:2816].transpose(1, 0, 2).reshape(r, 2304)
-    m = jnp.concatenate([gp[0, :, 2816:3456], gp[1, :, 2944:3456]], axis=1)
-    return qkv, a, i, m, gains[:, 0], gains[:, 1]
+    drain_all()
+
+
+frequency = np.broadcast_to(
+    (np.float32(rope_base) ** (-(np.arange(32, dtype=np.float32) * 2) / HEAD_DIM))[:, None], (32, 128)
+).astype(np.float32)
+
+
+def finish_kernel(lo_raw, gi_raw, gp, lo, gi, g_qkv, g_attn, g_in, g_mlp, g_one, g_two, buf, sem):
+    loads = [pltpu.make_async_copy(src, buf.at[i], sem.at[i]) for i, src in enumerate((lo_raw, gi_raw))]
+    stores = [pltpu.make_async_copy(buf.at[i], dst, sem.at[2 + i]) for i, dst in enumerate((lo, gi))]
+    for copy in loads:
+        copy.start()
+    for load, store in zip(loads, stores):
+        load.wait()
+        store.start()
+    for c in range(2):
+        for p in range(3):
+            for t in range(3):
+                o = 768 * t + 384 * c + 128 * p
+                at = PAIR + 384 * p + 128 * t
+                g_qkv[:, o : o + 128] = gp[c, :, at : at + 128]
+        g_attn[:, 384 * c : 384 * c + 384] = gp[c, :, ATTN : ATTN + 384]
+        g_in[:, 1152 * c : 1152 * c + 1152] = gp[c, :, IN : IN + 1152]
+    g_mlp[:, 0:640] = gp[0, :, MLP : MLP + 640]
+    g_mlp[:, 640:1152] = gp[1, :, MLP + 128 : MLP + 640]
+    both = gp[0, :, 0:128] + gp[1, :, 0:128]
+    flat = jnp.concatenate([both, jnp.zeros((104, 128), f32)], axis=0).T
+    g_one[...] = flat[0:1, 0:24]
+    g_two[...] = flat[1:2, 0:24]
+    for store in stores:
+        store.wait()
 
 
 def fast(layer_in, seg_start, out_grad, w_qkv, w_attn_out, w_in, w_mlp_out, norm_attn, norm_mlp):
-    wp = pack(w_qkv, w_attn_out, w_in, w_mlp_out, norm_attn, norm_mlp)
-    frequency = rope_base ** (-(jnp.arange(32).astype(f32) * 2.0) / HEAD_DIM)
-    freq = jnp.broadcast_to(frequency[:, None], (32, 128))
     hbm = pl.BlockSpec(memory_space=pltpu.HBM)
     vmem = pl.BlockSpec(memory_space=pltpu.VMEM)
     V = pltpu.VMEM
@@ -642,9 +747,11 @@
             jax.ShapeDtypeStruct((768, WIDTH), bf16),
             jax.ShapeDtypeStruct((6, 1024, 1024), bf16),
         ],
-        in_specs=[hbm, hbm, hbm, vmem, vmem],
+        in_specs=[hbm, hbm, vmem, hbm, hbm, hbm, hbm, vmem, vmem, vmem],
         out_specs=[hbm] * 5,
         scratch_shapes=[
+            V((2, 24, WIDTH), bf16),
+            V((8, 128), f32),
             V((1024, 768), bf16),
             V((1024, 768), bf16),
             V((1, 1024), jnp.int32),
@@ -688,14 +795,34 @@
             V((2, 24, WIDTH), bf16),
             V((2, 24, WIDTH), f32),
             pltpu.SemaphoreType.DMA((160,)),
-            pltpu.SemaphoreType.DMA((1,)),
+            pltpu.SemaphoreType.DMA((24,)),
             pltpu.SemaphoreType.DMA((220,)),
         ],
         compiler_params=pltpu.CompilerParams(
             collective_id=0, has_side_effects=True, vmem_limit_bytes=67043328
         ),
-    )(layer_in, out_grad, seg_start[:, None, :], wp, freq)
-    return (outs[0], outs[1], *unpack(outs[2]))
+    )(
+        layer_in, out_grad, seg_start, w_qkv, w_attn_out, w_in, w_mlp_out,
+        norm_attn[None], norm_mlp[None], frequency,
+    )
+    done = pl.pallas_call(
+        finish_kernel,
+        name="finish",
+        out_shape=[
+            jax.ShapeDtypeStruct((2, 256, 768), bf16),
+            jax.ShapeDtypeStruct((2, 256, 768), bf16),
+            jax.ShapeDtypeStruct((24, 2304), f32),
+            jax.ShapeDtypeStruct((24, 768), f32),
+            jax.ShapeDtypeStruct((24, 2304), f32),
+            jax.ShapeDtypeStruct((24, 1152), f32),
+            jax.ShapeDtypeStruct((1, 24), f32),
+            jax.ShapeDtypeStruct((1, 24), f32),
+        ],
+        in_specs=[hbm, hbm, vmem],
+        out_specs=[hbm, hbm] + [vmem] * 6,
+        scratch_shapes=[V((2, 2, 256, 768), bf16), pltpu.SemaphoreType.DMA((4,))],
+    )(*outs[:3])
+    return (*done[:6], done[6][0], done[7][0])
 
 
 def normalize(values):

time: 208 us -> 155 us (0.75)
  Pallas kernels: 184 us -> 154 us
  local copies, waits for them, and re-layouts: 20.3 us -> 0 us
  other arithmetic: 2.1 us -> 0 us
    pallas_call x1, Pallas kernels: 184 us -> 150 us  [fast(): pl.pallas_call(step_kernel, name='layer', out_shape=[jax.ShapeDtypeStruct...]
    unnamed x8 -> x0, local copies, waits for them, and re-layouts: 10.3 us -> none
    pallas_call x0 -> x1, Pallas kernels: none -> 4.22 us  [fast(): pl.pallas_call(finish_kernel, name='finish', out_shape=[jax.ShapeDtypeStr...]
    broadcast_in_dim x5 -> x0, local copies, waits for them, and re-layouts: 3.44 us -> none  [the longest x1 1.27 us: fast(): seg_start[:, None, :]]
    reshape x6 -> x0, local copies, waits for them, and re-layouts: 3.27 us -> none  [the longest x2 1.04 us: pack(): w_qkv.reshape(r, 3, 2, 3, 128).transpose(2, 0, 3, 1, 4).reshape(2, r, 1152)]
    squeeze x3 -> x0, local copies, waits for them, and re-layouts: 2.16 us -> none  [the longest x2 1.64 us: unpack(): m = jnp.concatenate([gp[0, :, 2816:3456], gp[1, :, 2944:3456]], axis=1)]
where the time goes in v2:
time: 155 us
  Pallas kernels  154 us (99%)
    pallas_call x1, Pallas kernels, fast(): pl.pallas_call(step_kernel, name='layer', out_shape=[jax.ShapeDtypeStruct...  150 us
    pallas_call x1, Pallas kernels, fast(): pl.pallas_call(finish_kernel, name='finish', out_shape=[jax.ShapeDtypeStr...  4.22 us

profile of v2, /device:TPU:0, one launch (start us, length us, event | category | flops | bytes accessed | tf_op | source)
XLA Modules:
  0.0 154.8 jit_solution(2843816371670133584)
XLA Ops:
  0.6 149.7 %layer.1 = (bf16[2,256,768]{2,1,0:T(8,128)(2,1)}, bf16[2,256,768]{2,1,0:T(8,128)(2,1)}, f32[2,24,3456]{2,1,0:T(8,128)}, bf16[768,3456]{1,0:T(8,128)(2,1)}, bf16[6,1024,1024]{2,1,0:T(8,128)(2,1)}) custom-call(bf16[2,256,768]{2,1,0:T(8,128)(2,1)} %x_in.1, bf16[2,256,768]{2,1,0:T(8,128)(2,1)} %dy_in.1, s32[2,256]{1,0:T(2,128)} %seg_in.1, ...), custom_call_target="tpu_custom_call" | custom-call | tf_op jit(solution)/shard_map/layer/pallas_call | solution.py:740
  150.4 4.2 %finish.1 = (bf16[2,256,768]{2,1,0:T(8,128)(2,1)}, bf16[2,256,768]{2,1,0:T(8,128)(2,1)}, f32[24,2304]{1,0:T(8,128)}, f32[24,768]{1,0:T(8,128)}, f32[24,2304]{1,0...) custom-call(bf16[2,256,768]{2,1,0:T(8,128)(2,1)} %get-tuple-element.19.lo_raw, ...), custom_call_target="tpu_custom_call" | custom-call | tf_op jit(solution)/shard_map/finish/pallas_call | solution.py:808

commit v3 on v2

--- a/solution.py
+++ b/solution.py
@@ -19,14 +19,14 @@
 norm_eps = 1e-05
 neg_large = -1e30
 
-WIDTH = 3456
-GATHER = [(0, 512), (512, 768), (1280, 384), (1664, 640), (2304, 512), (2816, 640)]
+WIDTH = 3328
+GATHER = [(0, 512), (512, 768), (1280, 384), (1664, 640), (2304, 512), (2816, 512)]
 PAIR = 128
 ATTN = 1280
 IN = 1664
 MLP = 2816
 REDUCE = {
-    "m": (2816, 640),
+    "m": (2816, 512),
     "i0": (1664, 640),
     "i1": (2304, 512),
     "a": (1280, 384),
@@ -67,7 +67,7 @@
     lo_out, gi_out, gp_out, land, keep,
     wp, gcol,
     xs, dys, sg, h1t, wq, wa, wi, wm, gains, cosr, sinr, qk, big, probs, otb, rl, x1, h2, hid, hidp,
-    dgo, dgp, dx1b, dx1bp, dot_send, dot_own, f1r, lo, gi, grad, grow, dkb, dvb,
+    dgo, dgp, dx1b, dx1bp, dot_send, dot_own, f1r, lo, gi, grad, grow, growp, dkb, dvb,
     ra, rb, ra2, rb2, zs, zp, zm, zx, fin,
     rs_, ls_, sends,
 ):
@@ -87,6 +87,8 @@
     qd = qx + 2 - 4 * (qx // 2)
     inner = jnp.logical_or(z == 1, z == 2)
     outer = jnp.logical_or(z == 0, z == 3)
+    near = k == zh
+    away = k != zh
     names = {}
     count = {"send": 0, "local": 0}
     drains = []
@@ -98,9 +100,16 @@
         index = view.transforms[0].indices
         return view.ref.at[tuple(pl.ds(0, at.size) if hasattr(at, "size") else 0 for at in index)]
 
-    def send(src, dst, name, dev, when=None, sem=None):
-        i = count["send"]
-        count["send"] += 1
+    keyed = {}
+
+    def send(src, dst, name, dev, when=None, sem=None, key=None):
+        first = key is None or key not in keyed
+        if first:
+            i = count["send"]
+            count["send"] += 1
+            keyed[key] = i
+        else:
+            i = keyed[key]
         copy = pltpu.make_async_remote_copy(
             src_ref=src, dst_ref=dst, send_sem=sends.at[i], recv_sem=rsem(name) if sem is None else sem,
             device_id=dev, device_id_type=MESH,
@@ -109,7 +118,8 @@
             copy.start()
         else:
             pl.when(when())(copy.start)
-        drains.append((i, src, when))
+        if first:
+            drains.append((i, src, when))
 
     def drain_all():
         for i, src, when in drains:
@@ -153,7 +163,8 @@
                 packs.append((w_qkv, 768 * t + 384 * c + 128 * p, c, PAIR + 384 * p + 128 * t, 128))
         packs.append((w_attn, 384 * c, c, ATTN, 384))
         packs.append((w_in, 1152 * c, c, IN, 1152))
-        packs.append((w_mlp, 512 * c, c, MLP, 640))
+        packs.append((w_mlp, 640 * c, c, MLP, 512))
+    packs.append((w_mlp, 512, 0, 0, 128))
     packing = [
         pltpu.make_async_copy(w.at[:, pl.ds(o, n)], wp.at[c, :, pl.ds(at, n)], ls_.at[i])
         for i, (w, o, c, at, n) in enumerate(packs)
@@ -164,32 +175,49 @@
     gcol[0:1, 0:24] = g_attn[...].astype(f32)
     gcol[1:2, 0:24] = g_mlp[...].astype(f32)
     columns = jnp.concatenate([gcol[...], jnp.zeros((120, 128), f32)], axis=0).T[0:24].astype(bf16)
-    wp[0, :, 0:128] = columns
     wp[1, :, 0:128] = columns
 
     @scoped
-    def zstage(u):
+    def zstage(u, turn=None):
         o, w = GATHER[u]
         cols = pl.ds(o, w)
-        dst = land.at[rows(dp * 96 + z * 24, 24), cols]
-        for c in range(2):
-            src = wp.at[c, :, cols]
-            send(src, dst, f"z{u}", (2 * q + c, zn))
-            send(src, dst, f"z{u}", (2 * q + c, zb))
-            send(src, dst, f"z{u}", (pn, z), when=lambda c=c: k != c)
-            pl.when(k == c)(lambda src=src: local(src, dst, f"z{u}") and None)
-
-    @scoped
-    def xystage(u):
+
+        def body():
+            dst = land.at[rows(dp * 96 + z * 24, 24), cols]
+            for c in range(2):
+                src = wp.at[c, :, cols]
+                send(src, dst, f"z{u}", (2 * q + c, zn), key=f"zn{u}{c}")
+                send(src, dst, f"z{u}", (2 * q + c, zb), key=f"zb{u}{c}")
+                send(src, dst, f"z{u}", (pn, z), when=lambda c=c: k != c, key=f"zp{u}{c}")
+                pl.when(k == c)(lambda src=src: local(src, dst, f"z{u}") and None)
+
+        in_turn(turn, body)
+
+    def in_turn(turn, body):
+        if turn is None:
+            body()
+        else:
+            pl.when(turn)(body)
+
+    @scoped
+    def slab_in(u, turn=None):
         o, w = GATHER[u]
         cols = pl.ds(o, w)
-        slab = land.at[rows(q * 192, 192), cols]
-        arrived(slab, f"z{u}")
+
+        def body():
+            arrived(land.at[rows(q * 192, 192), cols], f"z{u}")
+            for j in range(2):
+                part = land.at[rows((2 * q + j) * 96 + lax.rem(4 - 2 * z + 4, 4) * 24, 48), cols]
+                send(part, part, f"z{u}", (dp, zn), when=lambda: inner, key=f"fs{u}{j}")
+
+        in_turn(turn, body)
+
+    @scoped
+    def xysend(u):
+        o, w = GATHER[u]
+        slab = land.at[rows(q * 192, 192), pl.ds(o, w)]
         send(slab, slab, f"x{u}", (xn, z))
         send(slab, slab, f"y{u}", (yn, z))
-        for j in range(2):
-            part = land.at[rows((2 * q + j) * 96 + lax.rem(4 - 2 * z + 4, 4) * 24, 48), cols]
-            send(part, part, f"z{u}", (dp, zn), when=lambda: inner)
 
     @scoped
     def diag(u):
@@ -215,14 +243,14 @@
             dst = dst_ref.at[rows(z * 256, 256), :]
             sem = rs_.at[base[name] + lax.rem(z, 2)]
 
-            def away(m=m):
+            def going(m=m):
                 there = 2 * k + m != z
                 return there if turn is None else jnp.logical_and(turn, there)
 
             here = 2 * k + m == z
             if turn is not None:
                 here = jnp.logical_and(turn, here)
-            send(src, dst, None, (2 * q + zh, 2 * k + m), when=away, sem=sem)
+            send(src, dst, None, (2 * q + zh, 2 * k + m), when=going, sem=sem)
             pl.when(here)(pltpu.make_async_copy(src, dst, sem).start)
 
     base = {}
@@ -232,16 +260,22 @@
         names[name + "1"] = len(names)
 
     @scoped
-    def share_activation(ref, name):
-        for j in range(2):
-            r = rows(k * 512 + j * 256, 256)
-            arrived(ref.at[r, :], f"{name}{j}")
-            send(ref.at[r, :], ref.at[r, :], f"p{name}{j}", (pn, z))
-
-    @scoped
-    def shared_activation(ref, name):
-        for j in range(2):
-            arrived(ref.at[rows(other * 512 + j * 256, 256), :], f"p{name}{j}")
+    def share_activation(ref, name, turn=None):
+        def body():
+            for j in range(2):
+                r = rows(k * 512 + j * 256, 256)
+                arrived(ref.at[r, :], f"{name}{j}")
+                send(ref.at[r, :], ref.at[r, :], f"p{name}{j}", (pn, z), key=f"sh{name}{j}")
+
+        in_turn(turn, body)
+
+    @scoped
+    def shared_activation(ref, name, turn=None):
+        def body():
+            for j in range(2):
+                arrived(ref.at[rows(other * 512 + j * 256, 256), :], f"p{name}{j}")
+
+        in_turn(turn, body)
 
     @scoped
     def give_back(src_ref, out_ref, name, blocks=(0, 1)):
@@ -356,14 +390,21 @@
 
     for copy in packing:
         copy.wait()
-    for u in range(6):
-        zstage(u)
     seg_send()
-    activation(x_in, xs, "ax", outer)
-    xystage(0)
-    xystage(1)
-    xystage(2)
-    activation(x_in, xs, "ax", inner)
+    zstage(0)
+    zstage(1)
+    activation(x_in, xs, "ax", near)
+    zstage(2, outer)
+    zstage(3, outer)
+    slab_in(0)
+    xysend(0)
+    slab_in(1)
+    xysend(1)
+    zstage(2, inner)
+    zstage(3, inner)
+    slab_in(2, inner)
+    slab_in(3, inner)
+    activation(x_in, xs, "ax", away)
     arrived(sg, "seg")
     positions = (lax.broadcasted_iota(jnp.int32, (1, 1024), 1) - sg[...]).astype(f32)
     angles = freq[:, 0:1] * positions
@@ -379,51 +420,73 @@
         big[:, r] = jnp.where(column == here, 0.0, neg_large)
 
     diag(0)
-    xystage(3)
     diag(1)
-    xystage(4)
-    share_activation(xs, "ax")
+    slab_in(2, outer)
+    xysend(2)
+    zstage(4)
+    zstage(5)
     done(0)
-    local(land.at[:, pl.ds(0, 128)], gains, "cg")
+    first = land.at[:, pl.ds(0, 128)]
+    spare = wm.at[:, pl.ds(512, 128)]
+
+    @pl.when(k == 0)
+    def _():
+        local(first, spare, "cm")
+
+    @pl.when(k == 1)
+    def _():
+        local(first, gains, "cg")
+
+    send(first, spare, "cm", (pn, z), when=lambda: k == 0)
+    send(first, gains, "cg", (pn, z), when=lambda: k == 1)
     local(land.at[:, pl.ds(128, 384)], wq.at[0], "cq0")
     arrived(gains, "cg")
     gain_rows = gains[...].astype(f32).T
     grow[...] = gain_rows[0:8]
-    shared_activation(xs, "ax")
-
-    with scope("ln1"):
-        @pl.loop(0, 4)
-        def _(i):
-            xb = xs[rows(i * 256, 256), :].astype(f32)
-            c = xb - jnp.mean(xb, -1, keepdims=True)
-            n = c * lax.rsqrt(jnp.mean(c * c, -1, keepdims=True) + norm_eps)
-            h1t[:, lanes(i * 256, 256)] = (n * grow[0:1, :]).astype(bf16).T
-
     done(1)
     local(land.at[:, pl.ds(512, 384)], wq.at[1], "cq1")
     local(land.at[:, pl.ds(896, 384)], wq.at[2], "cq2")
+
+    def queries(half):
+        for i in range(2):
+            at = half * 512 + i * 256
+            xb = xs[rows(at, 256), :].astype(f32)
+            c = xb - jnp.mean(xb, -1, keepdims=True)
+            n = c * lax.rsqrt(jnp.mean(c * c, -1, keepdims=True) + norm_eps)
+            h1t[:, lanes(at, 256)] = (n * grow[0:1, :]).astype(bf16).T
+
+        cols = lanes(half * 512, 512)
+
+        @pl.loop(0, 3)
+        def _(p):
+            t = times(wq[p].T, h1t[:, cols])
+            c = cosr[:, cols]
+            s = sinr[:, cols]
+            for hh in range(4):
+                u1 = t[hh * 64 : hh * 64 + 32]
+                u2 = t[hh * 64 + 32 : hh * 64 + 64]
+                scale = HEAD_DIM**-0.5 if hh < 2 else 1.0
+                qk[p, hh * 64 : hh * 64 + 32, cols] = ((u1 * c - u2 * s) * scale).astype(bf16)
+                qk[p, hh * 64 + 32 : hh * 64 + 64, cols] = ((u2 * c + u1 * s) * scale).astype(bf16)
+            qk[p, 256:384, cols] = t[256:384].astype(bf16)
+
+    share_activation(xs, "ax", k == zh)
+    shared_activation(xs, "ax", k != zh)
     for p in range(3):
         arrived(wq.at[p], f"cq{p}")
-
-    @pl.loop(0, 3)
-    def _(p):
-        t = times(wq[p].T, h1t[...])
-        c = cosr[...]
-        s = sinr[...]
-        for hh in range(4):
-            u1 = t[hh * 64 : hh * 64 + 32]
-            u2 = t[hh * 64 + 32 : hh * 64 + 64]
-            scale = HEAD_DIM**-0.5 if hh < 2 else 1.0
-            qk[p, hh * 64 : hh * 64 + 32, :] = ((u1 * c - u2 * s) * scale).astype(bf16)
-            qk[p, hh * 64 + 32 : hh * 64 + 64, :] = ((u2 * c + u1 * s) * scale).astype(bf16)
-        qk[p, 256:384, :] = t[256:384].astype(bf16)
-
-        @pl.when(p == 1)
-        def _():
-            xystage(5)
-            activation(dy_in, dys, "ay")
-            diag(2)
-            diag(3)
+    slab_in(3, outer)
+    xysend(3)
+    with scope("qkvnear"):
+        queries(zh)
+    diag(2)
+    share_activation(xs, "ax", k != zh)
+    slab_in(4, inner)
+    shared_activation(xs, "ax", k == zh)
+    with scope("qkvfar"):
+        queries(1 - zh)
+    slab_in(5, inner)
+    slab_in(4, outer)
+    xysend(4)
 
     @scoped
     def weight_done(u):
@@ -437,8 +500,8 @@
             pieces = [(land.at[:, pl.ds(o, w)], wi.at[k, :, pl.ds(640, 512)], None)]
         else:
             pieces = [
-                (land.at[:, pl.ds(o, 640)], wm.at[:, pl.ds(0, 640)], lambda: k == 0),
-                (land.at[:, pl.ds(o + 128, 512)], wm.at[:, pl.ds(640, 512)], lambda: k == 1),
+                (land.at[:, pl.ds(o, w)], wm.at[:, pl.ds(0, 512)], lambda: k == 0),
+                (land.at[:, pl.ds(o, w)], wm.at[:, pl.ds(640, 512)], lambda: k == 1),
             ]
         for src, dst, when in pieces:
             if when is None:
@@ -456,7 +519,7 @@
         elif u == 4:
             mine, theirs = [(wi.at[k, :, pl.ds(640, 512)], None)], [(wi.at[other, :, pl.ds(640, 512)], None)]
         else:
-            low, high = wm.at[:, pl.ds(0, 640)], wm.at[:, pl.ds(640, 512)]
+            low, high = wm.at[:, pl.ds(0, 512)], wm.at[:, pl.ds(640, 512)]
             mine, theirs = [(low, k == 0), (high, k == 1)], [(low, k == 1), (high, k == 0)]
         for group, name in ((mine, "cw"), (theirs, "pw")):
             for ref, when in group:
@@ -471,11 +534,12 @@
     first_send = count["send"]
     count["send"] += 6
     forward_steps = {
-        0: lambda: diag(4),
-        1: lambda: (weight_done(2), diag(5)),
-        2: lambda: weight_done(3),
-        3: lambda: weight_done(4),
-        4: lambda: weight_done(5),
+        0: lambda: (slab_in(5, outer), xysend(5), activation(dy_in, dys, "ay"), diag(3)),
+        1: lambda: diag(4),
+        2: lambda: (weight_done(2), diag(5)),
+        3: lambda: weight_done(3),
+        4: lambda: weight_done(4),
+        5: lambda: weight_done(5),
     }
 
     @pl.loop(0, 6)
@@ -508,6 +572,7 @@
 
     for u in range(2, 6):
         weight_here(u)
+    arrived(spare, "cm")
     for h in range(6):
         arrived(otb.at[rows(other * 384 + h * 64, 64), :], f"o{h}")
     arrived(probs.at[0], "e4")
@@ -524,32 +589,47 @@
     n = c * lax.rsqrt(jnp.mean(c * c, -1, keepdims=True) + norm_eps)
     h2[mine, :] = (n * grow[1:2, :]).astype(bf16)
     send(h2.at[mine, :], h2.at[mine, :], "h2", (pn, z))
+    share_activation(dys, "ay")
     for o, w in ((0, 512), (512, 512), (1024, 128)):
         cols = pl.ds(o, w)
         a = times(h2[mine, :], wi[0, :, cols])
         b = times(h2[mine, :], wi[1, :, cols])
         phi = 0.5 * (1.0 + lax.erf(a * 0.7071067811865476))
         gelu = a * phi
+        e = times(dys[mine, :], wm[:, cols])
         hid[:, cols] = (gelu * b).astype(bf16)
-        big[0:512, cols] = b * (phi + a * (jnp.exp(-0.5 * a * a) * 0.3989422804014327))
-        big[512:1024, cols] = gelu
+        dgo[0, :, cols] = (e * (b * (phi + a * (jnp.exp(-0.5 * a * a) * 0.3989422804014327)))).astype(bf16)
+        dgo[1, :, cols] = (e * gelu).astype(bf16)
     send(hid.at[:, lanes(other * 512, 640)], hidp, "hid", (pn, z))
+    send(dgo.at[other], dgp, "dg", (pn, z))
+
+    shared_activation(dys, "ay")
+    arrived(hidp, "hid")
+    t = (
+        dims(dys[mine, :], hid[:, lanes(k * 512, 640)], 0, 0) + dims(dys[theirs, :], hidp[...], 0, 0)
+    ).astype(bf16)
+
+    @pl.when(k == 0)
+    def _():
+        grad[:, MLP : MLP + 512] = t[:, 0:512]
+        grad[:, 0:128] = t[:, 512:640]
+
+    @pl.when(k == 1)
+    def _():
+        grad[:, MLP : MLP + 512] = t[:, 128:640]
+
+    s1("m")
     lo[...] = (x1[...] + dims(hid[...], wm[...], 1, 1)).astype(bf16)
     give_back(lo, lo_out, "alo")
-
-    share_activation(dys, "ay")
-    shared_activation(dys, "ay")
-    arrived(hidp, "hid")
-    grad[:, MLP : MLP + 640] = (
-        dims(dys[mine, :], hid[:, lanes(k * 512, 640)], 0, 0) + dims(dys[theirs, :], hidp[...], 0, 0)
-    ).astype(bf16)
-    s1("m")
-    for o, w in ((0, 512), (512, 512), (1024, 128)):
+    arrived(h2.at[theirs, :], "h2")
+    arrived(dgp, "dg")
+    for name, o, w in (("i0", 0, 640), ("i1", 640, 512)):
         cols = pl.ds(o, w)
-        e = times(dys[mine, :], wm[:, cols])
-        dgo[0, :, cols] = (e * big[0:512, cols]).astype(bf16)
-        dgo[1, :, cols] = (e * big[512:1024, cols]).astype(bf16)
-    send(dgo.at[other], dgp, "dg", (pn, z))
+        grad[:, IN + o : IN + o + w] = (
+            dims(h2[mine, :], dgo[k, :, cols], 0, 0) + dims(h2[theirs, :], dgp[:, cols], 0, 0)
+        ).astype(bf16)
+        if name == "i0":
+            s1(name)
     f2 = dims(dgo[0], wi[0], 1, 1) + dims(dgo[1], wi[1], 1, 1)
     xx = x1[...]
     c = xx - jnp.mean(xx, -1, keepdims=True)
@@ -578,31 +658,22 @@
     local(keep.at[4], probs.at[0], "e4")
 
     s2("m")
-    arrived(h2.at[theirs, :], "h2")
-    arrived(dgp, "dg")
-    for name, o, w in (("i0", 0, 640), ("i1", 640, 512)):
-        cols = pl.ds(o, w)
-        grad[:, IN + o : IN + o + w] = (
-            dims(h2[mine, :], dgo[k, :, cols], 0, 0) + dims(h2[theirs, :], dgp[:, cols], 0, 0)
-        ).astype(bf16)
-        s1(name)
+    s1("i1")
     arrived(dx1bp, "dx1b")
     grad[:, ATTN : ATTN + 384] = (
         times(otb[:, my_lanes], dx1b[:, lanes(k * 384, 384)])
         + times(otb[:, lanes(other * 512, 512)], dx1bp[...])
     ).astype(bf16)
-    s1("a")
     arrived(dot_own.at[:, lanes(other * 512, 512)], "do")
 
     for h in range(6):
         rsem(f"b{h}")
     backward_steps = {
-        5: lambda: s3("m"),
-        4: lambda: (s1("q2"), s2("i0")),
-        3: lambda: (s2("i1"), s4("m")),
-        2: lambda: (s1("q1"), s2("a"), s5("m"), s3("i0")),
-        1: lambda: s2("q2"),
-        0: lambda: (s1("q0"), s4("i0"), s3("i1"), s3("a")),
+        4: lambda: (s2("i0"), s3("m")),
+        3: lambda: (s2("i1"), s1("a"), s1("q2")),
+        2: lambda: (s1("q1"), s3("i0"), s4("m")),
+        1: lambda: s3("i1"),
+        0: lambda: (s2("a"), s1("q0"), s4("i0")),
     }
 
     @pl.loop(0, 6)
@@ -658,12 +729,9 @@
 
     big[0:768, 0:512] = f1_part(lanes(other * 512, 512))
     send(big.at[pl.ds(0, 768), pl.ds(0, 512)], f1r, "f1", (pn, z))
+    s2("q2")
+    big[0:768, 512:1024] = f1_part(my_lanes)
     s4("i1")
-    big[0:768, 512:1024] = f1_part(my_lanes)
-    s3("q2")
-    s2("q1")
-    s5("i0")
-    s4("a")
     arrived(f1r, "f1")
     f1 = (big[0:768, 512:1024] + f1r[...]).T
     xx = xs[mine, :].astype(f32)
@@ -675,23 +743,35 @@
     gi[...] = (
         x1[...] + r1 * (cc - jnp.mean(cc, -1, keepdims=True) - n * jnp.mean(cc * n, -1, keepdims=True))
     ).astype(bf16)
-    two = jnp.concatenate([grow[2:4, :], jnp.zeros((126, 768), f32)], axis=0)
-    grad[:, 0:128] = two.T.astype(bf16)
+    send(grow, growp, "gr", (pn, z), when=lambda: k == 0)
+
+    @pl.when(k == 1)
+    def _():
+        arrived(growp, "gr")
+        two = jnp.concatenate([grow[2:4, :] + growp[2:4, :], jnp.zeros((126, 768), f32)], axis=0)
+        grad[:, 0:128] = two.T.astype(bf16)
+
     s1("g")
     give_back(gi, gi_out, "agi", (0,))
+    s2("q1")
+    s3("a")
+    s5("m")
+    give_back(gi, gi_out, "agi", (1,))
+    s2("q0")
+    s4("a")
+    s3("q2")
+    s2("g")
+    s3("q1")
+    s5("i0")
+    s3("q0")
     s4("q2")
-    s2("q0")
-    s3("q1")
+    s3("g")
+    s4("q1")
+    s4("q0")
     s5("i1")
     s5("a")
-    give_back(gi, gi_out, "agi", (1,))
-    s2("g")
-    s3("q0")
-    s4("q1")
-    s3("g")
+    s4("g")
     s5("q2")
-    s4("q0")
-    s4("g")
     s5("q1")
     s5("q0")
     s5("g")
@@ -700,6 +780,7 @@
     given_back(lo_out, "alo")
     given_back(gi_out, "agi")
     drain_all()
+    assert len(names) <= 160 and count["send"] <= 220 and len(packing) <= 32
 
 
 frequency = np.broadcast_to(
@@ -707,14 +788,19 @@
 ).astype(np.float32)
 
 
-def finish_kernel(lo_raw, gi_raw, gp, lo, gi, g_qkv, g_attn, g_in, g_mlp, g_one, g_two, buf, sem):
-    loads = [pltpu.make_async_copy(src, buf.at[i], sem.at[i]) for i, src in enumerate((lo_raw, gi_raw))]
-    stores = [pltpu.make_async_copy(buf.at[i], dst, sem.at[2 + i]) for i, dst in enumerate((lo, gi))]
+def finish_kernel(
+    lo_raw, gi_raw, gp_raw, lo, gi, o_qkv, o_attn, o_in, o_mlp, o_one, o_two,
+    buf, gp, g_qkv, g_attn, g_in, g_mlp, g_one, g_two, sem,
+):
+    loads = [
+        pltpu.make_async_copy(src, dst, sem.at[i])
+        for i, (src, dst) in enumerate(((gp_raw, gp), (lo_raw, buf.at[0]), (gi_raw, buf.at[1])))
+    ]
     for copy in loads:
         copy.start()
-    for load, store in zip(loads, stores):
-        load.wait()
-        store.start()
+    pairs = ((buf.at[0], lo), (buf.at[1], gi), (g_qkv, o_qkv), (g_attn, o_attn), (g_in, o_in), (g_mlp, o_mlp), (g_one, o_one), (g_two, o_two))
+    stores = [pltpu.make_async_copy(src, dst, sem.at[3 + i]) for i, (src, dst) in enumerate(pairs)]
+    loads[0].wait()
     for c in range(2):
         for p in range(3):
             for t in range(3):
@@ -723,12 +809,17 @@
                 g_qkv[:, o : o + 128] = gp[c, :, at : at + 128]
         g_attn[:, 384 * c : 384 * c + 384] = gp[c, :, ATTN : ATTN + 384]
         g_in[:, 1152 * c : 1152 * c + 1152] = gp[c, :, IN : IN + 1152]
-    g_mlp[:, 0:640] = gp[0, :, MLP : MLP + 640]
-    g_mlp[:, 640:1152] = gp[1, :, MLP + 128 : MLP + 640]
-    both = gp[0, :, 0:128] + gp[1, :, 0:128]
-    flat = jnp.concatenate([both, jnp.zeros((104, 128), f32)], axis=0).T
+    g_mlp[:, 0:512] = gp[0, :, MLP : MLP + 512]
+    g_mlp[:, 512:640] = gp[0, :, 0:128]
+    g_mlp[:, 640:1152] = gp[1, :, MLP : MLP + 512]
+    flat = jnp.concatenate([gp[1, :, 0:128], jnp.zeros((104, 128), f32)], axis=0).T
     g_one[...] = flat[0:1, 0:24]
     g_two[...] = flat[1:2, 0:24]
+    for load, store in zip(loads[1:], stores[:2]):
+        load.wait()
+        store.start()
+    for store in stores[2:]:
+        store.start()
     for store in stores:
         store.wait()
 
@@ -783,6 +874,7 @@
             V((512, 768), bf16),
             V((768, WIDTH), bf16),
             V((8, 768), f32),
+            V((8, 768), f32),
             V((64, 1024), f32),
             V((64, 1024), f32),
             V((2, 96, WIDTH), bf16),
@@ -795,7 +887,7 @@
             V((2, 24, WIDTH), bf16),
             V((2, 24, WIDTH), f32),
             pltpu.SemaphoreType.DMA((160,)),
-            pltpu.SemaphoreType.DMA((24,)),
+            pltpu.SemaphoreType.DMA((32,)),
             pltpu.SemaphoreType.DMA((220,)),
         ],
         compiler_params=pltpu.CompilerParams(
@@ -818,9 +910,19 @@
             jax.ShapeDtypeStruct((1, 24), f32),
             jax.ShapeDtypeStruct((1, 24), f32),
         ],
-        in_specs=[hbm, hbm, vmem],
-        out_specs=[hbm, hbm] + [vmem] * 6,
-        scratch_shapes=[V((2, 2, 256, 768), bf16), pltpu.SemaphoreType.DMA((4,))],
+        in_specs=[hbm, hbm, hbm],
+        out_specs=[hbm] * 8,
+        scratch_shapes=[
+            V((2, 2, 256, 768), bf16),
+            V((2, 24, WIDTH), f32),
+            V((24, 2304), f32),
+            V((24, 768), f32),
+            V((24, 2304), f32),
+            V((24, 1152), f32),
+            V((1, 24), f32),
+            V((1, 24), f32),
+            pltpu.SemaphoreType.DMA((11,)),
+        ],
     )(*outs[:3])
     return (*done[:6], done[6][0], done[7][0])
 

time: 155 us -> 147 us (0.948)
  Pallas kernels: 154 us -> 146 us
    pallas_call x1, Pallas kernels: 150 us -> 143 us  [fast(): pl.pallas_call(step_kernel, name='layer', out_shape=[jax.ShapeDtypeStruct...]
where the time goes in v3:
time: 147 us
  Pallas kernels  146 us (99%)
    pallas_call x1, Pallas kernels, fast(): pl.pallas_call(step_kernel, name='layer', out_shape=[jax.ShapeDtypeStruct...  143 us

profile of v3, /device:TPU:0, one launch (start us, length us, event | category | flops | bytes accessed | tf_op | source)
XLA Modules:
  0.0 146.9 jit_solution(16157615538701667967)
XLA Ops:
  0.6 143.3 %layer.1 = (bf16[2,256,768]{2,1,0:T(8,128)(2,1)}, bf16[2,256,768]{2,1,0:T(8,128)(2,1)}, f32[2,24,3328]{2,1,0:T(8,128)}, bf16[768,3328]{1,0:T(8,128)(2,1)}, bf16[6,1024,1024]{2,1,0:T(8,128)(2,1)}) custom-call(bf16[2,256,768]{2,1,0:T(8,128)(2,1)} %x_in.1, bf16[2,256,768]{2,1,0:T(8,128)(2,1)} %dy_in.1, s32[2,256]{1,0:T(2,128)} %seg_in.1, ...), custom_call_target="tpu_custom_call" | custom-call | tf_op jit(solution)/shard_map/layer/pallas_call | solution.py:831
  144.0 2.8 %finish.1 = (bf16[2,256,768]{2,1,0:T(8,128)(2,1)}, bf16[2,256,768]{2,1,0:T(8,128)(2,1)}, f32[24,2304]{1,0:T(8,128)}, f32[24,768]{1,0:T(8,128)}, f32[24,2304]{1,0...) custom-call(bf16[2,256,768]{2,1,0:T(8,128)(2,1)} %get-tuple-element.19.lo_raw, ...), custom_call_target="tpu_custom_call" | custom-call | tf_op jit(solution)/shard_map/finish/pallas_call | solution.py:900

commit v4 on v3

--- a/solution.py
+++ b/solution.py
@@ -278,18 +278,22 @@
         in_turn(turn, body)
 
     @scoped
-    def give_back(src_ref, out_ref, name, blocks=(0, 1)):
+    def give_back(src_ref, out_ref, name, blocks=(0, 1), turn=None):
         m = lax.rem(z, 2)
         for j in blocks:
             src = src_ref.at[pl.ds(j * 256, 256), :]
             dst = out_ref.at[m]
             sem = rs_.at[base[name] + m]
 
-            def away(j=j):
-                return jnp.logical_or(2 * k + j != z, zh != k)
-
-            send(src, dst, None, (2 * q + zh, 2 * k + j), when=away, sem=sem)
-            pl.when(jnp.logical_not(away()))(pltpu.make_async_copy(src, dst, sem).start)
+            def going(j=j):
+                leaves = jnp.logical_or(2 * k + j != z, zh != k)
+                return leaves if turn is None else jnp.logical_and(turn, leaves)
+
+            stays = jnp.logical_and(2 * k + j == z, zh == k)
+            if turn is not None:
+                stays = jnp.logical_and(turn, stays)
+            send(src, dst, None, (2 * q + zh, 2 * k + j), when=going, sem=sem)
+            pl.when(stays)(pltpu.make_async_copy(src, dst, sem).start)
 
     @scoped
     def given_back(out_ref, name):
@@ -402,9 +406,11 @@
     xysend(1)
     zstage(2, inner)
     zstage(3, inner)
+    zstage(4)
+    zstage(5)
+    activation(x_in, xs, "ax", away)
     slab_in(2, inner)
     slab_in(3, inner)
-    activation(x_in, xs, "ax", away)
     arrived(sg, "seg")
     positions = (lax.broadcasted_iota(jnp.int32, (1, 1024), 1) - sg[...]).astype(f32)
     angles = freq[:, 0:1] * positions
@@ -423,8 +429,6 @@
     diag(1)
     slab_in(2, outer)
     xysend(2)
-    zstage(4)
-    zstage(5)
     done(0)
     first = land.at[:, pl.ds(0, 128)]
     spare = wm.at[:, pl.ds(512, 128)]
@@ -474,19 +478,22 @@
     shared_activation(xs, "ax", k != zh)
     for p in range(3):
         arrived(wq.at[p], f"cq{p}")
+    slab_in(4, inner)
+    slab_in(5, inner)
     slab_in(3, outer)
     xysend(3)
     with scope("qkvnear"):
         queries(zh)
     diag(2)
+    slab_in(4, outer)
+    xysend(4)
     share_activation(xs, "ax", k != zh)
-    slab_in(4, inner)
     shared_activation(xs, "ax", k == zh)
     with scope("qkvfar"):
         queries(1 - zh)
-    slab_in(5, inner)
-    slab_in(4, outer)
-    xysend(4)
+    slab_in(5, outer)
+    xysend(5)
+    diag(3)
 
     @scoped
     def weight_done(u):
@@ -534,8 +541,7 @@
     first_send = count["send"]
     count["send"] += 6
     forward_steps = {
-        0: lambda: (slab_in(5, outer), xysend(5), activation(dy_in, dys, "ay"), diag(3)),
-        1: lambda: diag(4),
+        0: lambda: (activation(dy_in, dys, "ay"), diag(4)),
         2: lambda: (weight_done(2), diag(5)),
         3: lambda: weight_done(3),
         4: lambda: weight_done(4),
@@ -671,9 +677,9 @@
     backward_steps = {
         4: lambda: (s2("i0"), s3("m")),
         3: lambda: (s2("i1"), s1("a"), s1("q2")),
-        2: lambda: (s1("q1"), s3("i0"), s4("m")),
+        2: lambda: (s3("i0"), s4("m")),
         1: lambda: s3("i1"),
-        0: lambda: (s2("a"), s1("q0"), s4("i0")),
+        0: lambda: (s2("a"), s4("i0")),
     }
 
     @pl.loop(0, 6)
@@ -717,7 +723,7 @@
         qk[p, rows(160 + hh * 64, 32), :] = (d[32:] * c - d[:32] * s).astype(bf16)
         qk[p, vrow, :] = dvb[...].astype(bf16)
 
-        @pl.when(hh == 0)
+        @pl.when(h == 4)
         def _():
             grad[:, lanes(PAIR + 384 * p, 384)] = dims(h1t[...], qk[p], 1, 1).astype(bf16)
 
@@ -753,28 +759,33 @@
 
     s1("g")
     give_back(gi, gi_out, "agi", (0,))
+    give_back(gi, gi_out, "agi", (1,), inner)
+    for p in (1, 0):
+        grad[:, PAIR + 384 * p : PAIR + 384 * p + 384] = dims(h1t[...], qk[p], 1, 1).astype(bf16)
+        s1(f"q{p}")
+        if p == 1:
+            s3("a")
+    s3("q2")
+    s5("m")
+    s4("a")
     s2("q1")
-    s3("a")
-    s5("m")
-    give_back(gi, gi_out, "agi", (1,))
+    s2("g")
+    s4("q2")
+    s5("i0")
     s2("q0")
-    s4("a")
-    s3("q2")
-    s2("g")
+    s5("i1")
     s3("q1")
-    s5("i0")
+    s3("g")
     s3("q0")
-    s4("q2")
-    s3("g")
+    give_back(gi, gi_out, "agi", (1,), outer)
+    s5("a")
     s4("q1")
+    s4("g")
     s4("q0")
-    s5("i1")
-    s5("a")
-    s4("g")
     s5("q2")
     s5("q1")
+    s5("g")
     s5("q0")
-    s5("g")
     for u in REDUCE:
         s6(u)
     given_back(lo_out, "alo")

time: 147 us -> 143 us (0.973)
  Pallas kernels: 146 us -> 141 us
    pallas_call x1, Pallas kernels: 143 us -> 139 us  [fast(): pl.pallas_call(step_kernel, name='layer', out_shape=[jax.ShapeDtypeStruct...]
where the time goes in v4:
time: 143 us; the launch traced here: 142 us
  Pallas kernels  141 us (99%)
    pallas_call x1, Pallas kernels, fast(): pl.pallas_call(step_kernel, name='layer', out_shape=[jax.ShapeDtypeStruct...  139 us

profile of v4, /device:TPU:0, one launch (start us, length us, event | category | flops | bytes accessed | tf_op | source)
XLA Modules:
  0.0 142.3 jit_solution(10716051373046444417)
XLA Ops:
  0.6 138.7 %layer.1 = (bf16[2,256,768]{2,1,0:T(8,128)(2,1)}, bf16[2,256,768]{2,1,0:T(8,128)(2,1)}, f32[2,24,3328]{2,1,0:T(8,128)}, bf16[768,3328]{1,0:T(8,128)(2,1)}, bf16[6,1024,1024]{2,1,0:T(8,128)(2,1)}) custom-call(bf16[2,256,768]{2,1,0:T(8,128)(2,1)} %x_in.1, bf16[2,256,768]{2,1,0:T(8,128)(2,1)} %dy_in.1, s32[2,256]{1,0:T(2,128)} %seg_in.1, ...), custom_call_target="tpu_custom_call" | custom-call | tf_op jit(solution)/shard_map/layer/pallas_call | solution.py:842
  139.3 2.8 %finish.1 = (bf16[2,256,768]{2,1,0:T(8,128)(2,1)}, bf16[2,256,768]{2,1,0:T(8,128)(2,1)}, f32[24,2304]{1,0:T(8,128)}, f32[24,768]{1,0:T(8,128)}, f32[24,2304]{1,0...) custom-call(bf16[2,256,768]{2,1,0:T(8,128)(2,1)} %get-tuple-element.19.lo_raw, ...), custom_call_target="tpu_custom_call" | custom-call | tf_op jit(solution)/shard_map/finish/pallas_call | solution.py:911

commit v5 on v4

--- a/solution.py
+++ b/solution.py
@@ -63,9 +63,9 @@
 
 
 def step_kernel(
-    x_in, dy_in, seg_in, w_qkv, w_attn, w_in, w_mlp, g_attn, g_mlp, freq,
+    x_in, dy_in, seg_raw, w_qkv, w_attn, w_in, w_mlp, g_attn_raw, g_mlp_raw, freq_raw,
     lo_out, gi_out, gp_out, land, keep,
-    wp, gcol,
+    wp, gcol, seg_in, g_attn, g_mlp, freq,
     xs, dys, sg, h1t, wq, wa, wi, wm, gains, cosr, sinr, qk, big, probs, otb, rl, x1, h2, hid, hidp,
     dgo, dgp, dx1b, dx1bp, dot_send, dot_own, f1r, lo, gi, grad, grow, growp, dkb, dvb,
     ra, rb, ra2, rb2, zs, zp, zm, zx, fin,
@@ -169,9 +169,17 @@
         pltpu.make_async_copy(w.at[:, pl.ds(o, n)], wp.at[c, :, pl.ds(at, n)], ls_.at[i])
         for i, (w, o, c, at, n) in enumerate(packs)
     ]
-    for copy in packing:
+    small = [
+        pltpu.make_async_copy(src, dst, ls_.at[len(packs) + i])
+        for i, (src, dst) in enumerate(
+            ((g_attn_raw, g_attn), (g_mlp_raw, g_mlp), (seg_raw, seg_in), (freq_raw, freq))
+        )
+    ]
+    for copy in small + packing:
         copy.start()
     gcol[...] = jnp.zeros_like(gcol)
+    for copy in small:
+        copy.wait()
     gcol[0:1, 0:24] = g_attn[...].astype(f32)
     gcol[1:2, 0:24] = g_mlp[...].astype(f32)
     columns = jnp.concatenate([gcol[...], jnp.zeros((120, 128), f32)], axis=0).T[0:24].astype(bf16)
@@ -544,8 +552,7 @@
         0: lambda: (activation(dy_in, dys, "ay"), diag(4)),
         2: lambda: (weight_done(2), diag(5)),
         3: lambda: weight_done(3),
-        4: lambda: weight_done(4),
-        5: lambda: weight_done(5),
+        4: lambda: (weight_done(4), weight_done(5)),
     }
 
     @pl.loop(0, 6)
@@ -609,6 +616,8 @@
     send(hid.at[:, lanes(other * 512, 640)], hidp, "hid", (pn, z))
     send(dgo.at[other], dgp, "dg", (pn, z))
 
+    lo[...] = (x1[...] + dims(hid[...], wm[...], 1, 1)).astype(bf16)
+    give_back(lo, lo_out, "alo")
     shared_activation(dys, "ay")
     arrived(hidp, "hid")
     t = (
@@ -625,8 +634,6 @@
         grad[:, MLP : MLP + 512] = t[:, 128:640]
 
     s1("m")
-    lo[...] = (x1[...] + dims(hid[...], wm[...], 1, 1)).astype(bf16)
-    give_back(lo, lo_out, "alo")
     arrived(h2.at[theirs, :], "h2")
     arrived(dgp, "dg")
     for name, o, w in (("i0", 0, 640), ("i1", 640, 512)):
@@ -735,8 +742,8 @@
 
     big[0:768, 0:512] = f1_part(lanes(other * 512, 512))
     send(big.at[pl.ds(0, 768), pl.ds(0, 512)], f1r, "f1", (pn, z))
+    big[0:768, 512:1024] = f1_part(my_lanes)
     s2("q2")
-    big[0:768, 512:1024] = f1_part(my_lanes)
     s4("i1")
     arrived(f1r, "f1")
     f1 = (big[0:768, 512:1024] + f1r[...]).T
@@ -791,7 +798,7 @@
     given_back(lo_out, "alo")
     given_back(gi_out, "agi")
     drain_all()
-    assert len(names) <= 160 and count["send"] <= 220 and len(packing) <= 32
+    assert len(names) <= 160 and count["send"] <= 220 and len(packing) + len(small) <= 32
 
 
 frequency = np.broadcast_to(
@@ -837,7 +844,6 @@
 
 def fast(layer_in, seg_start, out_grad, w_qkv, w_attn_out, w_in, w_mlp_out, norm_attn, norm_mlp):
     hbm = pl.BlockSpec(memory_space=pltpu.HBM)
-    vmem = pl.BlockSpec(memory_space=pltpu.VMEM)
     V = pltpu.VMEM
     outs = pl.pallas_call(
         step_kernel,
@@ -849,11 +855,15 @@
             jax.ShapeDtypeStruct((768, WIDTH), bf16),
             jax.ShapeDtypeStruct((6, 1024, 1024), bf16),
         ],
-        in_specs=[hbm, hbm, vmem, hbm, hbm, hbm, hbm, vmem, vmem, vmem],
+        in_specs=[hbm] * 10,
         out_specs=[hbm] * 5,
         scratch_shapes=[
             V((2, 24, WIDTH), bf16),
             V((8, 128), f32),
+            V((2, 256), jnp.int32),
+            V((1, 24), bf16),
+            V((1, 24), bf16),
+            V((32, 128), f32),
             V((1024, 768), bf16),
             V((1024, 768), bf16),
             V((1, 1024), jnp.int32),

time: 143 us -> 141 us (0.986)
  no operation moved by 1% of the time
where the time goes in v5:
time: 141 us
  Pallas kernels  140 us (99%)
    pallas_call x1, Pallas kernels, fast(): pl.pallas_call(step_kernel, name='layer', out_shape=[jax.ShapeDtypeStruct...  138 us

profile of v5, /device:TPU:0, one launch (start us, length us, event | category | flops | bytes accessed | tf_op | source)
XLA Modules:
  0.0 141.2 jit_solution(12543126038761146876)
XLA Ops:
  0.6 137.6 %layer.1 = (bf16[2,256,768]{2,1,0:T(8,128)(2,1)}, bf16[2,256,768]{2,1,0:T(8,128)(2,1)}, f32[2,24,3328]{2,1,0:T(8,128)}, bf16[768,3328]{1,0:T(8,128)(2,1)}, bf16[6,1024,1024]{2,1,0:T(8,128)(2,1)}) custom-call(bf16[2,256,768]{2,1,0:T(8,128)(2,1)} %x_in.1, bf16[2,256,768]{2,1,0:T(8,128)(2,1)} %dy_in.1, s32[2,256]{1,0:T(2,128)} %seg_raw.1, ...), custom_call_target="tpu_custom_call" | custom-call | tf_op jit(solution)/shard_map/layer/pallas_call | solution.py:848
  138.2 2.8 %finish.1 = (bf16[2,256,768]{2,1,0:T(8,128)(2,1)}, bf16[2,256,768]{2,1,0:T(8,128)(2,1)}, f32[24,2304]{1,0:T(8,128)}, f32[24,768]{1,0:T(8,128)}, f32[24,2304]{1,0...) custom-call(bf16[2,256,768]{2,1,0:T(8,128)(2,1)} %get-tuple-element.19.lo_raw, ...), custom_call_target="tpu_custom_call" | custom-call | tf_op jit(solution)/shard_map/finish/pallas_call | solution.py:921

commit v6 on v5

--- a/solution.py
+++ b/solution.py
@@ -246,13 +246,14 @@
         arrived(land.at[rows(qd * 192 + 96, 96), cols], f"dy{u}")
 
     def activation(src_ref, dst_ref, name, turn=None):
-        for m in range(2):
+        for j in range(2):
+            m = j + k - 2 * j * k
             src = src_ref.at[m]
             dst = dst_ref.at[rows(z * 256, 256), :]
             sem = rs_.at[base[name] + lax.rem(z, 2)]
 
-            def going(m=m):
-                there = 2 * k + m != z
+            def going(j=j):
+                there = 2 * k + j + k - 2 * j * k != z
                 return there if turn is None else jnp.logical_and(turn, there)
 
             here = 2 * k + m == z

time: 141 us -> 142 us (level)
  no operation moved by 1% of the time
where the time goes in v6:
time: 142 us
  Pallas kernels  141 us (99%)
    pallas_call x1, Pallas kernels, fast(): pl.pallas_call(step_kernel, name='layer', out_shape=[jax.ShapeDtypeStruct...  138 us

profile of v6, /device:TPU:0, one launch (start us, length us, event | category | flops | bytes accessed | tf_op | source)
XLA Modules:
  0.0 141.6 jit_solution(3212398053167474752)
XLA Ops:
  0.6 138.0 %layer.1 = (bf16[2,256,768]{2,1,0:T(8,128)(2,1)}, bf16[2,256,768]{2,1,0:T(8,128)(2,1)}, f32[2,24,3328]{2,1,0:T(8,128)}, bf16[768,3328]{1,0:T(8,128)(2,1)}, bf16[6,1024,1024]{2,1,0:T(8,128)(2,1)}) custom-call(bf16[2,256,768]{2,1,0:T(8,128)(2,1)} %x_in.1, bf16[2,256,768]{2,1,0:T(8,128)(2,1)} %dy_in.1, s32[2,256]{1,0:T(2,128)} %seg_raw.1, ...), custom_call_target="tpu_custom_call" | custom-call | tf_op jit(solution)/shard_map/layer/pallas_call | solution.py:849
  138.7 2.8 %finish.1 = (bf16[2,256,768]{2,1,0:T(8,128)(2,1)}, bf16[2,256,768]{2,1,0:T(8,128)(2,1)}, f32[24,2304]{1,0:T(8,128)}, f32[24,768]{1,0:T(8,128)}, f32[24,2304]{1,0...) custom-call(bf16[2,256,768]{2,1,0:T(8,128)(2,1)} %get-tuple-element.19.lo_raw, ...), custom_call_target="tpu_custom_call" | custom-call | tf_op jit(solution)/shard_map/finish/pallas_call | solution.py:922
